TPU v7x, 256 devices: a whole 4x4x8 slice. The times are simulated.
256 devices in a mesh: dp: 16 (over z, core), sx: 4 (over y), sy: 4 (over x).
Axes of the slice: x: 4, y: 4, z: 8, core: 2. Of those that a mesh axis runs over, the one named last changes fastest.
Arguments:
- volume: bfloat16 [16, 32, 32, 32, 128], P('dp', None, 'sx', 'sy'), may hold values from -6 to 6
- conv_one: bfloat16 [16, 32, 32, 32, 128], P('dp', None, 'sx', 'sy'), may hold values from -300 to 300
- conv_two: bfloat16 [16, 32, 32, 32, 128], P('dp', None, 'sx', 'sy'), may hold values from -300 to 300
- upper_grad: bfloat16 [16, 32, 32, 32, 128], P('dp', None, 'sx', 'sy'), may hold values from -36 to 36
- weight_one: bfloat16 [3, 3, 3, 32, 32], replicated, may hold values from -0.21875 to 0.21875
- weight_two: bfloat16 [3, 3, 3, 32, 32], replicated, may hold values from -0.21875 to 0.21875
- gain_one: float32 [32], replicated, may hold values from 0.1 to 1.9
- bias_one: float32 [32], replicated, may hold values from -1 to 1
- gain_two: float32 [32], replicated, may hold values from 0.1 to 1.9
- bias_two: float32 [32], replicated, may hold values from -1 to 1
Outputs:
- input_grad: bfloat16 [16, 32, 32, 32, 128], P('dp', None, 'sx', 'sy')
- weight_one_grad: float32 [3, 3, 3, 32, 32], replicated
- weight_two_grad: float32 [3, 3, 3, 32, 32], replicated
- gain_one_grad: float32 [32], replicated
- bias_one_grad: float32 [32], replicated
- gain_two_grad: float32 [32], replicated
- bias_two_grad: float32 [32], replicated
All inputs are finite; a program needn't handle non-finite values.
Results may differ from a plain program's by a relative error of at most 0.014.
Values may be sent and summed in bfloat16 or wider, within the bound.
No kernel may reach another device: no remote copies, remote signals or barrier semaphores. Data moves between devices by JAX's collectives and lax.ppermute only.
A program may use at most 64 MiB of HBM per device.

v0:
```python
import functools
import math

import jax
import jax.numpy as jnp
from jax import lax
from jax.experimental import pallas as pl
from jax.experimental.pallas import tpu as pltpu
from jax.sharding import Mesh
from jax.sharding import PartitionSpec as P

DP = ("dp_0", "dp_1")
ALL = ("dp_0", "dp_1", "sx", "sy")
PLANE = ("dp_1", "sx", "sy")
EPS = 1e-05
F32 = jnp.float32
BF16 = jnp.bfloat16
C = 32
B = 8
Z = 128
CELLS = float(16 * 32 * 32 * Z)
SCALE = 1.0 / math.sqrt(CELLS)

SIDES = tuple((dx, dy) for dx in (-1, 0, 1) for dy in (-1, 0, 1) if (dx, dy) != (0, 0))
VMEM = pltpu.MemorySpace.VMEM
SMEM = pltpu.MemorySpace.SMEM


def span(d, width):
    if d == 0:
        return range(B)
    return range(B - width, B) if d > 0 else range(width)


def landing(d, width):
    if d == 0:
        return range(width, B + width)
    return range(B + width, B + 2 * width) if d > 0 else range(width)


def slabs(side):
    out = []
    for which, width in (("c2", 2), ("ug", 2), ("c1", 1)):
        for x in span(side[0], width):
            for y in span(side[1], width):
                out.append((which, x, y))
    return out


def places(side):
    out = []
    for which, width in (("c2", 2), ("ug", 2), ("c1", 1)):
        for x in landing(side[0], width):
            for y in landing(side[1], width):
                out.append((which, x, y))
    return out


def call(kernel, outs, scratch=(), flops=0, n_smem=0, n_in=0):
    single = not isinstance(outs, (list, tuple))
    shapes = [outs] if single else list(outs)
    f = pl.pallas_call(
        kernel,
        out_shape=shapes[0] if single else tuple(shapes),
        in_specs=[pl.BlockSpec(memory_space=SMEM)] * n_smem
        + [pl.BlockSpec(memory_space=VMEM)] * (n_in - n_smem),
        out_specs=pl.BlockSpec(memory_space=VMEM)
        if single
        else tuple(pl.BlockSpec(memory_space=VMEM) for _ in shapes),
        scratch_shapes=list(scratch),
        compiler_params=pltpu.CompilerParams(vmem_limit_bytes=40 * 2**20),
        cost_estimate=pl.CostEstimate(flops=flops, bytes_accessed=1 << 20, transcendentals=0),
    )
    return f


def shaped(dims, kind):
    return jax.ShapeDtypeStruct(dims, kind)


def across(columns):
    return jnp.sum(jnp.transpose(columns), axis=0, keepdims=True)


def down(row):
    return jnp.transpose(jnp.broadcast_to(row, (128, 128)))


def arrived(ref):
    total = jnp.sum(ref[...].reshape(ref.shape[0], 128), axis=0, keepdims=True)
    return total


def stats_kernel(one_ref, two_ref, out_ref):
    parts = []
    for ref in (one_ref, two_ref):
        sums, squares = [], []
        for c in range(C):
            block = ref[0, c].astype(F32)
            sums.append(jnp.sum(jnp.sum(block, axis=0), axis=0, keepdims=True))
            squares.append(jnp.sum(jnp.sum(block * block, axis=0), axis=0, keepdims=True))
        parts += [jnp.concatenate(sums, 0), jnp.concatenate(squares, 0)]
    row = across(jnp.concatenate(parts, 0))
    out_ref[...] = jnp.broadcast_to(row[None], out_ref.shape)


def shifted(slab, lane):
    before = jnp.where(lane == 0, 0.0, pltpu.roll(slab, 1, axis=1))
    after = jnp.where(lane == Z - 1, 0.0, pltpu.roll(slab, Z - 1, axis=1))
    return jnp.concatenate([before, slab, after], 0)


def lanes():
    return lax.broadcasted_iota(jnp.int32, (C, Z), 1)


def spread_kernel(one_ref, two_ref, up_ref, vol_ref, c1_ref, c2_ref, ug_ref, vol3_ref, *rest):
    sends, tmp = rest[:-1], rest[-1]
    lane = lanes()
    wanted = {}
    for n, side in enumerate(SIDES):
        for i, key in enumerate(slabs(side)):
            wanted.setdefault(key, []).append((n, i))
    for name, src, dst in (("c1", one_ref, c1_ref), ("c2", two_ref, c2_ref), ("ug", up_ref, ug_ref), ("vol", vol_ref, None)):
        tmp[...] = src[0].reshape(C * B * B, Z).astype(F32)
        for x in range(B):
            for y in range(B):
                slab = tmp[pl.ds(x * B + y, C, stride=B * B), :]
                if name == "vol":
                    vol3_ref[x, :, y * Z : (y + 1) * Z] = shifted(slab, lane).astype(BF16)
                    continue
                small = slab.astype(BF16)
                dst[x, :, y * Z : (y + 1) * Z] = small
                for n, i in wanted.get((name, x, y), ()):
                    sends[n][i] = small


def extend_kernel(pos_ref, c1_ref, c2_ref, ug_ref, vol3_ref, *rest):
    received = rest[:8]
    c1x_ref, c2x_ref, ugx_ref, r_ref, marks = rest[8:]
    for ref, own, w in ((c1x_ref, c1_ref, 1), (c2x_ref, c2_ref, 2), (ugx_ref, ug_ref, 2)):
        for x in range(B):
            ref[x + w, :, w * Z : (w + B) * Z] = own[x]
    target = {"c1": c1x_ref, "c2": c2x_ref, "ug": ugx_ref}
    for n, side in enumerate(SIDES):
        for i, (which, x, y) in enumerate(places(side)):
            target[which][x, :, y * Z : (y + 1) * Z] = received[n][i]
    sx, sy = pos_ref[0], pos_ref[1]
    row = lax.broadcasted_iota(jnp.int32, (16, B * Z), 0)
    gy = sy * B + lax.broadcasted_iota(jnp.int32, (16, B * Z), 1) // Z
    wy = gy + 1 - row % 3
    ok_y = (wy >= 0) & (wy < 4 * B) & (row < 9)

    def body(x, acc):
        wx = sx * B + x + 1 - row // 3
        ok = ok_y & (wx >= 0) & (wx < 4 * B)
        inside = jnp.where(ok, 1.0, 0.0).astype(BF16)
        parts = []
        for kx in range(3):
            for ky in range(3):
                parts.append(c1x_ref[x + 2 - kx, :, (2 - ky) * Z : (2 - ky + B) * Z])
        parts.append(inside)
        rhs = jnp.concatenate(parts, 0)
        return acc + lax.dot_general(
            vol3_ref[x], rhs, (((1,), (1,)), ((), ())), preferred_element_type=F32
        )

    acc = lax.fori_loop(0, B, body, jnp.zeros((3 * C, 9 * C + 16), F32))
    r_ref[...] = jnp.concatenate([acc, jnp.zeros((3 * C, 384 - 9 * C - 16), F32)], 1)


def moments(total, squares):
    mean = total * (1.0 / CELLS)
    inv = lax.rsqrt(squares * (1.0 / CELLS) - mean * mean + EPS)
    return mean, inv


def sigmoid(v):
    return 0.5 * jnp.tanh(0.5 * v) + 0.5


def silu_slope(v):
    s = sigmoid(v)
    return s * (1.0 + v * (1.0 - s))


def sums_two_kernel(got_ref, par_ref, c2_ref, ug_ref, out_ref, norm_ref, row_ref):
    row = arrived(got_ref)
    row_ref[...] = jnp.broadcast_to(row, (8, 128))
    cols = down(row)
    mean1, inv1 = moments(cols[0:32], cols[32:64])
    mean2, inv2 = moments(cols[64:96], cols[96:128])
    norm_ref[0], norm_ref[1], norm_ref[2], norm_ref[3] = mean1, inv1, mean2, inv2
    gain, bias = par_ref[64:96], par_ref[96:128]

    def body(x, acc):
        b, g = acc
        for y in range(B):
            cent = (c2_ref[x, :, y * Z : (y + 1) * Z].astype(F32) - mean2) * inv2
            up = ug_ref[x, :, y * Z : (y + 1) * Z].astype(F32)
            slope = up * silu_slope(gain * cent + bias)
            b, g = b + slope, g + slope * cent
        return b, g

    zero = jnp.zeros((C, Z), F32)
    b, g = lax.fori_loop(0, B, body, (zero, zero))
    out = across(jnp.concatenate([b, g, zero, zero], 0))
    out_ref[...] = jnp.broadcast_to(out[None], out_ref.shape)


def activation_kernel(norm_ref, par_ref, c1_ref, act3_ref):
    mean, inv = norm_ref[0], norm_ref[1]
    gain, bias = par_ref[0:32], par_ref[32:64]
    lane = lanes()

    def body(x, carry):
        for y in range(B):
            cent = (c1_ref[x, :, y * Z : (y + 1) * Z].astype(F32) - mean) * inv
            pre = gain * cent + bias
            act = (pre * sigmoid(pre)).astype(BF16).astype(F32)
            act3_ref[x, :, y * Z : (y + 1) * Z] = shifted(act, lane).astype(BF16)
        return carry

    lax.fori_loop(0, B, body, 0)


def edge(index, width, side, low, high):
    if index < width:
        return low
    if index >= width + B:
        return high
    return None


def windows(ref, x, first, y_first, count):
    parts = []
    for kx in range(3):
        for ky in range(3):
            parts.append(ref[x + first - kx, :, (y_first - ky) * Z : (y_first - ky + count) * Z])
    return jnp.concatenate(parts, 0)


def unshift(t, y, lane):
    left = t[0:C, y * Z : (y + 1) * Z]
    mid = t[C : 2 * C, y * Z : (y + 1) * Z]
    right = t[2 * C : 3 * C, y * Z : (y + 1) * Z]
    out = mid + jnp.where(lane == Z - 1, 0.0, pltpu.roll(left, Z - 1, axis=1))
    return out + jnp.where(lane == 0, 0.0, pltpu.roll(right, 1, axis=1))


def three(value):
    hi = value.astype(BF16).astype(F32)
    mid = (value - hi).astype(BF16).astype(F32)
    lo = value - hi - mid
    return hi, mid, lo


def middle_kernel(
    pos_ref, got_ref, norm_ref, par_ref, w_ref, c1x_ref, c2x_ref, ugx_ref, vol3_ref, act3_ref, r_ref,
    msg_ref, slope_ref, row_ref, grad, msg,
):
    sx, sy = pos_ref[0], pos_ref[1]
    row = arrived(got_ref)
    row_ref[...] = jnp.broadcast_to(row, (8, 128))
    cols = down(row)
    mean1, inv1, mean2, inv2 = norm_ref[0], norm_ref[1], norm_ref[2], norm_ref[3]
    gain1, bias1, gain2, bias2 = par_ref[0:32], par_ref[32:64], par_ref[64:96], par_ref[96:128]
    b2, g2 = cols[0:32] * (1.0 / CELLS), cols[32:64] * (1.0 / CELLS)
    amp = gain2 * inv2
    lane = lanes()
    inside_y = {
        y: jnp.where(sy > 0, 1.0, 0.0) if y < 2 else jnp.where(sy < 3, 1.0, 0.0)
        for y in (0, 1, B + 2, B + 3)
    }

    def first(x, carry):
        gx = sx * B + x - 2
        inside_x = jnp.where((gx >= 0) & (gx < 4 * B), 1.0, 0.0)
        amp_x = amp * inside_x
        for y in range(B + 4):
            cent = (c2x_ref[x, :, y * Z : (y + 1) * Z].astype(F32) - mean2) * inv2
            up = ugx_ref[x, :, y * Z : (y + 1) * Z].astype(F32)
            slope = up * silu_slope(gain2 * cent + bias2)
            a = amp_x * inside_y[y] if y in inside_y else amp_x
            grad[x, :, y * Z : (y + 1) * Z] = (a * (slope - b2 - cent * g2)).astype(BF16)
        return carry

    lax.fori_loop(0, B + 4, first, 0)
    inside_y = {0: jnp.where(sy > 0, 1.0, 0.0), B + 1: jnp.where(sy < 3, 1.0, 0.0)}

    def second(x, acc):
        b, g = acc
        gx = sx * B + x - 1
        inside_x = jnp.where((gx >= 0) & (gx < 4 * B), 1.0, 0.0)
        own_x = jnp.where((x >= 1) & (x <= B), 1.0, 0.0)
        t = jnp.dot(w_ref[...], windows(grad, x, 2, 2, B + 2), preferred_element_type=F32)
        bx, gsum = jnp.zeros((C, Z), F32), jnp.zeros((C, Z), F32)
        for y in range(B + 2):
            cent = (c1x_ref[x, :, y * Z : (y + 1) * Z].astype(F32) - mean1) * inv1
            slope = unshift(t, y, lane) * silu_slope(gain1 * cent + bias1)
            if 1 <= y <= B:
                bx, gsum = bx + slope, gsum + slope * cent
            inside = inside_x * inside_y[y] if y in inside_y else inside_x
            slope_ref[x, :, y * Z : (y + 1) * Z] = (slope * inside).astype(BF16)
        return b + bx * own_x, g + gsum * own_x

    zero = jnp.zeros((C, Z), F32)
    b, g = lax.fori_loop(0, B + 2, second, (zero, zero))

    def third(x, acc):
        s, f = acc
        dims = (((1,), (1,)), ((), ()))
        s = s + lax.dot_general(
            vol3_ref[x], windows(slope_ref, x, 2, 2, B), dims, preferred_element_type=F32
        )
        f = f + lax.dot_general(
            act3_ref[x], windows(grad, x, 3, 3, B), dims, preferred_element_type=F32
        )
        return s, f

    empty = jnp.zeros((3 * C, 9 * C), F32)
    s, f = lax.fori_loop(0, B, third, (empty, empty))
    pad = jnp.zeros((3 * C, 384 - 9 * C), F32)
    sums = across(jnp.concatenate([b, g, zero, zero], 0))
    hi, mid, lo = three(sums)
    for m, part in enumerate((jnp.concatenate([s, pad], 1), r_ref[...], jnp.concatenate([f, pad], 1))):
        for kz in range(3):
            for t in range(3):
                msg[:, m * 9 + kz * 3 + t, :] = part[kz * C : (kz + 1) * C, t * 128 : (t + 1) * 128]
    for i, part in enumerate((hi, mid, lo)):
        msg[:, 27 + i, :] = jnp.broadcast_to(part, (C, 128))
    msg[:, 30, :] = zero
    msg[:, 31, :] = zero
    msg_ref[...] = msg[...].astype(BF16)


def relay_kernel(got_ref, out_ref):
    total = jnp.sum(got_ref[...].astype(F32), axis=0)
    sums = total[27:28] + total[28:29] + total[29:30]
    hi, mid, lo = three(sums)
    out = jnp.concatenate([total[0:27], hi, mid, lo, total[30:32]], 0).astype(BF16)
    out_ref[...] = jnp.broadcast_to(out[None], out_ref.shape)


def share_kernel(got_ref, stat_ref, lanepar_ref, out_ref, row_ref):
    total = jnp.sum(got_ref[...].astype(F32), axis=0)
    sums = total[27:28] + total[28:29] + total[29:30]
    row_ref[...] = jnp.broadcast_to(sums, (8, 128))
    lane = lax.broadcasted_iota(jnp.int32, (1, 128), 1)
    stat = stat_ref[0:1]
    mean = stat * (1.0 / CELLS)
    squares = pltpu.roll(stat, 96, axis=1) * (1.0 / CELLS)
    inv = lax.rsqrt(jnp.where(lane < C, squares - mean * mean, 0.0) + EPS)
    g = pltpu.roll(sums, 96, axis=1)
    alpha = lanepar_ref[0:1] * inv
    gamma = alpha * inv * g * (1.0 / CELLS)
    delta = alpha * sums * (1.0 / CELLS) - gamma * mean
    rows = jnp.where(lane < C, jnp.concatenate([alpha, gamma, delta], 0), 0.0)
    rows = jnp.concatenate([rows, jnp.zeros((5, 128), F32)], 0)
    a = lax.broadcasted_iota(jnp.int32, (128, 384), 0)
    o = lax.broadcasted_iota(jnp.int32, (128, 384), 1)
    tile = jnp.where(o % C == a, 1.0, 0.0)
    wide = jnp.dot(rows, tile, precision=lax.Precision.HIGHEST, preferred_element_type=F32)
    spread = jnp.where((o // C + C == a) & (o < 9 * C), 1.0, 0.0)
    marks = jnp.concatenate([total[11:12], total[14:15], total[17:18], jnp.zeros((5, 128), F32)], 0)
    ones = jnp.dot(marks, spread, precision=lax.Precision.HIGHEST, preferred_element_type=F32)
    parts = []
    for kz in range(3):
        for t in range(3):
            cut = slice(t * 128, (t + 1) * 128)
            one = (
                wide[0:1, cut] * total[kz * 3 + t : kz * 3 + t + 1]
                - wide[1:2, cut] * total[9 + kz * 3 + t : 10 + kz * 3 + t]
                - wide[2:3, cut] * ones[kz : kz + 1, cut]
            )
            parts.append(one)
    out = jnp.concatenate(parts + [total[18:27], jnp.zeros((6, 128), F32)], 0) * SCALE
    out_ref[...] = jnp.broadcast_to(out.astype(BF16)[None], out_ref.shape)


def last_kernel(sum_ref, norm_ref, par_ref, w_ref, mask_ref, c1x_ref, slope_ref, out_ref, grad, tmp):
    cols = down(sum_ref[0:1])
    mean, inv = norm_ref[0], norm_ref[1]
    b, g = cols[0:32] * (1.0 / CELLS), cols[32:64] * (1.0 / CELLS)
    amp = par_ref[0:32] * inv
    lane = lanes()
    sx, sy = mask_ref[0], mask_ref[1]
    inside_y = {0: jnp.where(sy > 0, 1.0, 0.0), B + 1: jnp.where(sy < 3, 1.0, 0.0)}

    def first(x, carry):
        gx = sx * B + x - 1
        amp_x = amp * jnp.where((gx >= 0) & (gx < 4 * B), 1.0, 0.0)
        for y in range(B + 2):
            cent = (c1x_ref[x, :, y * Z : (y + 1) * Z].astype(F32) - mean) * inv
            slope = slope_ref[x, :, y * Z : (y + 1) * Z].astype(F32)
            a = amp_x * inside_y[y] if y in inside_y else amp_x
            grad[x, :, y * Z : (y + 1) * Z] = (a * (slope - b - cent * g)).astype(BF16)
        return carry

    lax.fori_loop(0, B + 2, first, 0)

    for x in range(B):
        t = jnp.dot(w_ref[...], windows(grad, x, 2, 2, B), preferred_element_type=F32)
        for y in range(B):
            tmp[pl.ds(x * B + y, C, stride=B * B), :] = unshift(t, y, lane)
    out_ref[0] = tmp[...].astype(BF16).reshape(C, B, B, Z)


def filters_kernel(got_ref, one_ref, two_ref, tmp):
    tmp[...] = got_ref[...].astype(F32)
    for m, ref in enumerate((one_ref, two_ref)):
        for kz in range(3):
            for t in range(3):
                slab = tmp[:, m * 9 + kz * 3 + t, :]
                for i in range(4):
                    k = 4 * t + i
                    if k < 9:
                        ref[k // 3, k % 3, kz] = slab[:, i * C : (i + 1) * C]


def exchanged(array, axes):
    return lax.all_to_all(array, axes, 0, 0, tiled=True)


def per_device(
    volume, conv_one, conv_two, upper_grad, weight_one, weight_two, gain_one, bias_one, gain_two, bias_two
):
    pos = jnp.stack([lax.axis_index("sx"), lax.axis_index("sy")]).astype(jnp.int32)
    packed = jnp.concatenate([gain_one, bias_one, gain_two, bias_two])
    par = jnp.broadcast_to(packed[:, None], (128, 128))
    lanepar = jnp.broadcast_to(packed[None, :], (8, 128))
    w_one = jnp.transpose(weight_one, (2, 3, 0, 1, 4)).reshape(3 * C, 9 * C)
    w_two = jnp.transpose(weight_two, (2, 3, 0, 1, 4)).reshape(3 * C, 9 * C)
    everyone = shaped((256, 1, 128), F32)

    stats = call(stats_kernel, everyone, n_in=2)(conv_one, conv_two)
    got_stats = exchanged(stats, ALL)

    block = shaped((B, C, B * Z), BF16)
    spread = call(
        spread_kernel,
        [block, block, block, shaped((B, 3 * C, B * Z), BF16)]
        + [shaped((len(slabs(side)), C, Z), BF16) for side in SIDES],
        scratch=[pltpu.VMEM((C * B * B, Z), F32)],
        flops=3 * 10**9,
        n_in=4,
    )(conv_one, conv_two, upper_grad, volume)
    c1, c2, ug, vol3 = spread[:4]
    received = []
    for n, (dx, dy) in enumerate(SIDES):
        pairs = []
        for x in range(4):
            for y in range(4):
                if 0 <= x + dx < 4 and 0 <= y + dy < 4:
                    pairs.append(((x + dx) * 4 + y + dy, x * 4 + y))
        message = spread[4 + SIDES.index((-dx, -dy))]
        received.append(lax.ppermute(message, ("sx", "sy"), pairs))
    c1x, c2x, ugx, r = call(
        extend_kernel,
        [
            shaped((B + 2, C, (B + 2) * Z), BF16),
            shaped((B + 4, C, (B + 4) * Z), BF16),
            shaped((B + 4, C, (B + 4) * Z), BF16),
            shaped((3 * C, 384), F32),
        ],
        scratch=[pltpu.VMEM((16, B * Z), BF16)],
        flops=3 * 10**9,
        n_smem=1,
        n_in=13,
    )(pos, c1, c2, ug, vol3, *received)

    sums_two, norm, stat_row = call(
        sums_two_kernel,
        [everyone, shaped((4, C, Z), F32), shaped((8, 128), F32)],
        flops=10**9,
        n_in=4,
    )(got_stats, par, c2, ug)
    got_two = exchanged(sums_two, ALL)
    act3 = call(activation_kernel, shaped((B, 3 * C, B * Z), BF16), flops=10**9, n_in=3)(norm, par, c1)

    terms, slope, row_two = call(
        middle_kernel,
        [
            shaped((32, 32, 128), BF16),
            shaped((B + 2, C, (B + 2) * Z), BF16),
            shaped((8, 128), F32),
        ],
        scratch=[pltpu.VMEM((B + 4, C, (B + 4) * Z), BF16), pltpu.VMEM((32, 32, 128), F32)],
        flops=4 * 10**9,
        n_smem=1,
        n_in=11,
    )(pos, got_two, norm, par, w_two, c1x, c2x, ugx, vol3, act3, r)

    relay = call(relay_kernel, shaped((8, 32, 128), BF16), n_in=1)(exchanged(terms, PLANE))
    shares, row_one = call(
        share_kernel, [shaped((32, 24, 128), BF16), shaped((8, 128), F32)], n_in=3
    )(exchanged(relay, "dp_0"), stat_row, lanepar)
    got_shares = exchanged(shares, PLANE)
    input_grad = call(
        lambda sum_ref, *refs: last_kernel(sum_ref, *refs[0:3], refs[3], *refs[4:]),
        shaped((1, C, B, B, Z), BF16),
        scratch=[pltpu.VMEM((B + 2, C, (B + 2) * Z), BF16), pltpu.VMEM((C * B * B, Z), F32)],
        flops=4 * 10**9,
        n_in=7,
    ) if False else None
    input_grad = pl.pallas_call(
        last_kernel,
        out_shape=shaped((1, C, B, B, Z), BF16),
        in_specs=[pl.BlockSpec(memory_space=VMEM)] * 4
        + [pl.BlockSpec(memory_space=SMEM)]
        + [pl.BlockSpec(memory_space=VMEM)] * 2,
        out_specs=pl.BlockSpec(memory_space=VMEM),
        scratch_shapes=[pltpu.VMEM((B + 2, C, (B + 2) * Z), BF16), pltpu.VMEM((C * B * B, Z), F32)],
        compiler_params=pltpu.CompilerParams(vmem_limit_bytes=40 * 2**20),
        cost_estimate=pl.CostEstimate(flops=4 * 10**9, bytes_accessed=1 << 20, transcendentals=0),
    )(row_one, norm, par, w_one, pos, c1x, slope)
    filters = shaped((3, 3, 3, C, C), F32)
    filter_one, filter_two = call(
        filters_kernel, [filters, filters], scratch=[pltpu.VMEM((32, 24, 128), F32)], n_in=1
    )(got_shares)
    one = row_one[0] * SCALE
    two = row_two[0] * SCALE
    return (input_grad, filter_one, filter_two, one[32:64], one[0:32], two[32:64], two[0:32])


def solution(mesh):
    finer = Mesh(
        mesh.devices.reshape(8, 2, mesh.shape["sx"], mesh.shape["sy"]), ("dp_0", "dp_1", "sx", "sy")
    )
    field = P(DP, None, "sx", "sy", None)
    return jax.shard_map(
        per_device,
        mesh=finer,
        in_specs=(field,) * 4 + (P(),) * 6,
        out_specs=(field,) + (P(),) * 6,
        check_vma=False,
    )
```

profile of v0, /device:TPU:1, one launch (start us, length us, event | category | flops | bytes accessed | tf_op | source)
XLA Modules:
  0.0 156.3 jit_solution(2895098234866812121)
XLA Ops:
  2.7 1.2 shard_map.153
  3.9 15.6 %all-to-all-start = ((f32[256,1,128]{2,1,0:T(1,128)}), f32[256,1,128]{2,1,0:T(1,128)S(1)}, u32[]{:S(2)}, u32[]{:S(2)}) async-start(f32[256,1,128]{2,1,0:T(1,128)} %shard_map.153), calls=%async_computation | async-start | bytes 262144 | tf_op jit(solution)/shard_map/all_to_all | solution.py:422
  23.7 3.4 %shard_map.154 = (bf16[8,32,1024]{2,1,0:T(8,128)(2,1)S(1)}, bf16[8,32,1024]{2,1,0:T(8,128)(2,1)S(1)}, bf16[8,32,1024]{2,1,0:T(8,128)(2,1)S(1)}, bf16[8,96,1024]{...) custom-call(bf16[1,32,8,8,128]{4,3,2,1,0:T(8,128)(2,1)S(1)} %copy-do, ...), custom_call_target="tpu_custom_call" | custom-call | flops 3000000000 | bytes 1048576 | tf_op jit(solution)/shard_map/pallas_call | solution.py:440
  29.5 1.2 copy-done.16
  30.7 3.3 %collective-permute-start.1 = (bf16[40,32,128]{2,1,0:T(8,128)(2,1)S(1)}, bf16[40,32,128]{2,1,0:T(8,128)(2,1)S(1)}, u32[]{:S(2)}, u32[]{:S(2)}) collective-permute-start(bf16[40,32,128]{2,1,0:T(8,128)(2,1)S(1)} %get-tuple-element.40), channel_id=1, source_target_pairs={{0,4},{1,5},{2,6},{3,7},{4,8},{5,9},{6,10},{7,11},{8,12},{9,13},{1... | collective-permute-start | bytes 983048 | tf_op jit(solution)/shard_map/ppermute | solution.py:457
  34.0 3.1 %collective-permute-start.3 = (bf16[40,32,128]{2,1,0:T(8,128)(2,1)S(1)}, bf16[40,32,128]{2,1,0:T(8,128)(2,1)S(1)}, u32[]{:S(2)}, u32[]{:S(2)}) collective-permute-start(bf16[40,32,128]{2,1,0:T(8,128)(2,1)S(1)} %get-tuple-element.42), channel_id=1, source_target_pairs={{0,1},{1,2},{2,3},{4,5},{5,6},{6,7},{8,9},{9,10},{10,11},{12,13},{... | collective-permute-start | bytes 983048 | tf_op jit(solution)/shard_map/ppermute | solution.py:457
  37.1 1.3 collective-permute-start.4
  38.4 1.3 collective-permute-start.6
  39.7 5.8 %collective-permute-start = (bf16[9,32,128]{2,1,0:T(8,128)(2,1)S(1)}, bf16[9,32,128]{2,1,0:T(8,128)(2,1)S(1)}, u32[]{:S(2)}, u32[]{:S(2)}) collective-permute-start(bf16[9,32,128]{2,1,0:T(8,128)(2,1)S(1)} %get-tuple-element.39), channel_id=1, source_target_pairs={{0,5},{1,6},{2,7},{4,9},{5,10},{6,11},{8,13},{9,14},{10,15},{16,21... | collective-permute-start | bytes 221192 | tf_op jit(solution)/shard_map/ppermute | solution.py:457
  45.6 1.1 copy.19
  48.4 1.0 copy-done.11
  50.5 1.8 %shard_map.155 = (f32[256,1,128]{2,1,0:T(1,128)}, f32[4,32,128]{2,1,0:T(8,128)S(1)}, f32[8,128]{1,0:T(8,128)S(1)}) custom-call(f32[256,1,128]{2,1,0:T(1,128)S(1)} %all-to-all-done.got_ref, f32[128,128]{1,0:T(8,128)S(1)} %broadcast_in_dim.4.par_ref, bf16[8,32,1024]{2,1,0:T(8,128)(2,1)S(1)} %copy-done.11, bf16[8,32,1024]{2,1,0:T(8,128)(2,1)S(1)} %copy-done.14), custom_call_target="tpu_custom_call" | custom-call | flops 1000000000 | bytes 1048576 | tf_op jit(solution)/shard_map/pallas_call | solution.py:472
  52.3 24.0 %all-to-all-start.1 = ((f32[256,1,128]{2,1,0:T(1,128)}), f32[256,1,128]{2,1,0:T(1,128)S(1)}, u32[]{:S(2)}, u32[]{:S(2)}) async-start(f32[256,1,128]{2,1,0:T(1,128)} %get-tuple-element.35), calls=%async_computation.1 | async-start | bytes 262144 | tf_op jit(solution)/shard_map/all_to_all | solution.py:422
  76.3 1.3 collective-permute-start.7
  78.6 1.1 shard_map.157.act3_ref
  79.7 1.1 copy-done.6
  80.8 1.9 %collective-permute-done.7.rest_7_ = bf16[9,32,128]{2,1,0:T(8,128)(2,1)S(1)} collective-permute-done((bf16[9,32,128]{2,1,0:T(8,128)(2,1)S(1)}, bf16[9,32,128]{2,1,0:T(8,128)(2,1)S(1)}, u32[]{:S(2)}, u32[]{:S(2)}) %collective-permute-start.7) | collective-permute-done | bytes 73760 | tf_op jit(solution)/shard_map/ppermute | solution.py:457
  82.8 3.8 %shard_map.156 = (bf16[10,32,1280]{2,1,0:T(8,128)(2,1)S(1)}, bf16[12,32,1536]{2,1,0:T(8,128)(2,1)S(1)}, bf16[12,32,1536]{2,1,0:T(8,128)(2,1)S(1)}, f32[96,384]{1,0:T(8,128)S(1)}) custom-call(s32[2]{0:T(128)S(1)} %pad_add_fusion.pos_ref.mask_ref, bf16[8,32,1024]{2,1,0:T(8,128)(2,1)S(1)} %copy-done.9, bf16[8,32,1024]{2,1,0:T(8,128)(2,1)S(1)} %copy-done.12, ...), custom_call_target="tpu_custom_call" | custom-call | flops 3000000000 | bytes 1048576 | tf_op jit(solution)/shard_map/pallas_call | solution.py:458
  89.7 1.4 copy-done.7
  91.1 1.4 copy-done.18
  92.5 1.3 copy-done.20
  93.7 1.3 copy-done.22
  95.0 1.1 copy-done.24
  96.2 12.0 %shard_map.158 = (bf16[32,32,128]{2,1,0:T(8,128)(2,1)}, bf16[10,32,1280]{2,1,0:T(8,128)(2,1)S(1)}, f32[8,128]{1,0:T(8,128)S(1)}) custom-call(s32[2]{0:T(128)S(1)} %pad_add_fusion.pos_ref.mask_ref, f32[256,1,128]{2,1,0:T(1,128)S(1)} %all-to-all-done.1.got_ref, f32[4,32,128]{2,1,0:T(8,128)S(1)} %get-tuple-element.36.norm_ref, ...), custom_call_target="tpu_custom_call" | custom-call | flops 4000000000 | bytes 1048576 | tf_op jit(solution)/shard_map/pallas_call | solution.py:481
  108.1 8.6 %all-to-all-start.2 = ((bf16[32,32,128]{2,1,0:T(8,128)(2,1)}), bf16[32,32,128]{2,1,0:T(8,128)(2,1)S(1)}, u32[]{:S(2)}, u32[]{:S(2)}) async-start(bf16[32,32,128]{2,1,0:T(8,128)(2,1)} %get-tuple-element.51), calls=%async_computation.2 | async-start | bytes 524288 | tf_op jit(solution)/shard_map/all_to_all | solution.py:422
  117.2 8.0 %all-to-all-done.2.got_ref = bf16[32,32,128]{2,1,0:T(8,128)(2,1)S(1)} async-done(((bf16[32,32,128]{2,1,0:T(8,128)(2,1)}), bf16[32,32,128]{2,1,0:T(8,128)(2,1)S(1)}, u32[]{:S(2)}, u32[]{:S(2)}) %all-to-all-start.2) | async-done | bytes 262176 | tf_op jit(solution)/shard_map/all_to_all | solution.py:422
  125.8 7.0 %all-to-all-start.3 = ((bf16[8,32,128]{2,1,0:T(8,128)(2,1)}), bf16[8,32,128]{2,1,0:T(8,128)(2,1)S(1)}, u32[]{:S(2)}, u32[]{:S(2)}) async-start(bf16[8,32,128]{2,1,0:T(8,128)(2,1)} %shard_map.159), calls=%async_computation.3 | async-start | bytes 131072 | tf_op jit(solution)/shard_map/all_to_all | solution.py:422
  133.4 6.6 %all-to-all-done.3.got_ref = bf16[8,32,128]{2,1,0:T(8,128)(2,1)S(1)} async-done(((bf16[8,32,128]{2,1,0:T(8,128)(2,1)}), bf16[8,32,128]{2,1,0:T(8,128)(2,1)S(1)}, u32[]{:S(2)}, u32[]{:S(2)}) %all-to-all-start.3) | async-done | bytes 65568 | tf_op jit(solution)/shard_map/all_to_all | solution.py:422
  141.0 6.1 %all-to-all-start.4 = ((bf16[32,24,128]{2,1,0:T(8,128)(2,1)}), bf16[32,24,128]{2,1,0:T(8,128)(2,1)S(1)}, u32[]{:S(2)}, u32[]{:S(2)}) async-start(bf16[32,24,128]{2,1,0:T(8,128)(2,1)} %get-tuple-element.55), calls=%async_computation.4 | async-start | bytes 393216 | tf_op jit(solution)/shard_map/all_to_all | solution.py:422
  147.1 4.0 %shard_map.161 = bf16[1,32,8,8,128]{4,3,2,1,0:T(8,128)(2,1)} custom-call(f32[8,128]{1,0:T(8,128)S(1)} %get-tuple-element.53.sum_ref, f32[4,32,128]{2,1,0:T(8,128)S(1)} %get-tuple-element.36.norm_ref, f32[128,128]{1,0:T(8,128)S(1)} %broadcast_in_dim.4.par_ref, bf16[96,288]{1,0:T(8,128)(2,1)S(1)} %reshape.31.w_ref, s32[2]{0:T(128)S(1)} %pad_add_fusion.pos_ref.mask_ref, ...), custom_call_target="tpu_custom_call" | custom-call | flops 4000000000 | bytes 1048576 | tf_op jit(solution)/shard_map/pallas_call | solution.py:506
  151.7 3.5 %all-to-all-done.4.got_ref = bf16[32,24,128]{2,1,0:T(8,128)(2,1)S(1)} async-done(((bf16[32,24,128]{2,1,0:T(8,128)(2,1)}), bf16[32,24,128]{2,1,0:T(8,128)(2,1)S(1)}, u32[]{:S(2)}, u32[]{:S(2)}) %all-to-all-start.4) | async-done | bytes 196640 | tf_op jit(solution)/shard_map/all_to_all | solution.py:422
  155.2 1.1 shard_map.162
  (78 shorter events, 18.7 us)
Async XLA Ops:
  3.9 44.4 %all-to-all-start = ((f32[256,1,128]{2,1,0:T(1,128)}), f32[256,1,128]{2,1,0:T(1,128)S(1)}, u32[]{:S(2)}, u32[]{:S(2)}) async-start(f32[256,1,128]{2,1,0:T(1,128)} %shard_map.153), calls=%async_computation | async-start | bytes 262144 | tf_op jit(solution)/shard_map/all_to_all | solution.py:422
  19.5 1.0 copy-start.1
  23.7 23.8 %copy-start.27 = (f32[32]{0:T(128)S(1)}, f32[32]{0:T(128)}, u32[]{:S(2)}) copy-start(f32[32]{0:T(128)} %param.19) | copy-start | bytes 388
  23.7 23.8 %copy-start.28 = (f32[32]{0:T(128)S(1)}, f32[32]{0:T(128)}, u32[]{:S(2)}) copy-start(f32[32]{0:T(128)} %param.18) | copy-start | bytes 388
  23.7 23.8 %copy-start.29 = (f32[32]{0:T(128)S(1)}, f32[32]{0:T(128)}, u32[]{:S(2)}) copy-start(f32[32]{0:T(128)} %param.17) | copy-start | bytes 388
  23.7 23.8 %copy-start.30 = (f32[32]{0:T(128)S(1)}, f32[32]{0:T(128)}, u32[]{:S(2)}) copy-start(f32[32]{0:T(128)} %param.16) | copy-start | bytes 388
  29.5 1.2 copy-start.16
  30.7 52.1 %collective-permute-start.1 = (bf16[40,32,128]{2,1,0:T(8,128)(2,1)S(1)}, bf16[40,32,128]{2,1,0:T(8,128)(2,1)S(1)}, u32[]{:S(2)}, u32[]{:S(2)}) collective-permute-start(bf16[40,32,128]{2,1,0:T(8,128)(2,1)S(1)} %get-tuple-element.40), channel_id=1, source_target_pairs={{0,4},{1,5},{2,6},{3,7},{4,8},{5,9},{6,10},{7,11},{8,12},{9,13},{1... | collective-permute-start | bytes 983048 | tf_op jit(solution)/shard_map/ppermute | solution.py:457
  34.0 48.8 %collective-permute-start.3 = (bf16[40,32,128]{2,1,0:T(8,128)(2,1)S(1)}, bf16[40,32,128]{2,1,0:T(8,128)(2,1)S(1)}, u32[]{:S(2)}, u32[]{:S(2)}) collective-permute-start(bf16[40,32,128]{2,1,0:T(8,128)(2,1)S(1)} %get-tuple-element.42), channel_id=1, source_target_pairs={{0,1},{1,2},{2,3},{4,5},{5,6},{6,7},{8,9},{9,10},{10,11},{12,13},{... | collective-permute-start | bytes 983048 | tf_op jit(solution)/shard_map/ppermute | solution.py:457
  37.1 45.7 %collective-permute-start.4 = (bf16[40,32,128]{2,1,0:T(8,128)(2,1)S(1)}, bf16[40,32,128]{2,1,0:T(8,128)(2,1)S(1)}, u32[]{:S(2)}, u32[]{:S(2)}) collective-permute-start(bf16[40,32,128]{2,1,0:T(8,128)(2,1)S(1)} %get-tuple-element.43), channel_id=1, source_target_pairs={{1,0},{2,1},{3,2},{5,4},{6,5},{7,6},{9,8},{10,9},{11,10},{13,12},{... | collective-permute-start | bytes 983048 | tf_op jit(solution)/shard_map/ppermute | solution.py:457
  38.4 44.4 %collective-permute-start.6 = (bf16[40,32,128]{2,1,0:T(8,128)(2,1)S(1)}, bf16[40,32,128]{2,1,0:T(8,128)(2,1)S(1)}, u32[]{:S(2)}, u32[]{:S(2)}) collective-permute-start(bf16[40,32,128]{2,1,0:T(8,128)(2,1)S(1)} %get-tuple-element.45), channel_id=1, source_target_pairs={{4,0},{5,1},{6,2},{7,3},{8,4},{9,5},{10,6},{11,7},{12,8},{13,9},{1... | collective-permute-start | bytes 983048 | tf_op jit(solution)/shard_map/ppermute | solution.py:457
  39.7 7.2 %collective-permute-start = (bf16[9,32,128]{2,1,0:T(8,128)(2,1)S(1)}, bf16[9,32,128]{2,1,0:T(8,128)(2,1)S(1)}, u32[]{:S(2)}, u32[]{:S(2)}) collective-permute-start(bf16[9,32,128]{2,1,0:T(8,128)(2,1)S(1)} %get-tuple-element.39), channel_id=1, source_target_pairs={{0,5},{1,6},{2,7},{4,9},{5,10},{6,11},{8,13},{9,14},{10,15},{16,21... | collective-permute-start | bytes 221192 | tf_op jit(solution)/shard_map/ppermute | solution.py:457
  46.9 0.8 collective-permute-start.2
  47.6 28.6 %collective-permute-start.5 = (bf16[9,32,128]{2,1,0:T(8,128)(2,1)S(1)}, bf16[9,32,128]{2,1,0:T(8,128)(2,1)S(1)}, u32[]{:S(2)}, u32[]{:S(2)}) collective-permute-start(bf16[9,32,128]{2,1,0:T(8,128)(2,1)S(1)} %get-tuple-element.44), channel_id=1, source_target_pairs={{4,1},{5,2},{6,3},{8,5},{9,6},{10,7},{12,9},{13,10},{14,11},{20,17... | collective-permute-start | bytes 221192 | tf_op jit(solution)/shard_map/ppermute | solution.py:457
  48.4 1.1 copy-start.11
  52.3 37.4 %all-to-all-start.1 = ((f32[256,1,128]{2,1,0:T(1,128)}), f32[256,1,128]{2,1,0:T(1,128)S(1)}, u32[]{:S(2)}, u32[]{:S(2)}) async-start(f32[256,1,128]{2,1,0:T(1,128)} %get-tuple-element.35), calls=%async_computation.1 | async-start | bytes 262144 | tf_op jit(solution)/shard_map/all_to_all | solution.py:422
  76.3 6.5 %collective-permute-start.7 = (bf16[9,32,128]{2,1,0:T(8,128)(2,1)S(1)}, bf16[9,32,128]{2,1,0:T(8,128)(2,1)S(1)}, u32[]{:S(2)}, u32[]{:S(2)}) collective-permute-start(bf16[9,32,128]{2,1,0:T(8,128)(2,1)S(1)} %get-tuple-element.46), channel_id=1, source_target_pairs={{5,0},{6,1},{7,2},{9,4},{10,5},{11,6},{13,8},{14,9},{15,10},{21,16... | collective-permute-start | bytes 221192 | tf_op jit(solution)/shard_map/ppermute | solution.py:457
  78.6 4.2 %copy-start.12 = (bf16[8,32,1024]{2,1,0:T(8,128)(2,1)S(1)}, bf16[8,32,1024]{2,1,0:T(8,128)(2,1)}, u32[]{:S(2)}) copy-start(bf16[8,32,1024]{2,1,0:T(8,128)(2,1)} %copy-done.10) | copy-start | bytes 1572868
  78.6 4.2 %copy-start.15 = (bf16[8,32,1024]{2,1,0:T(8,128)(2,1)S(1)}, bf16[8,32,1024]{2,1,0:T(8,128)(2,1)}, u32[]{:S(2)}) copy-start(bf16[8,32,1024]{2,1,0:T(8,128)(2,1)} %copy-done.13) | copy-start | bytes 1572868
  78.6 4.2 %copy-start.17 = (bf16[8,96,1024]{2,1,0:T(8,128)(2,1)S(1)}, bf16[8,96,1024]{2,1,0:T(8,128)(2,1)}, u32[]{:S(2)}) copy-start(bf16[8,96,1024]{2,1,0:T(8,128)(2,1)} %copy-done.16) | copy-start | bytes 4718596
  79.7 1.1 copy-start.6
  87.7 1.0 copy-start.21
  89.7 1.4 copy-start.7
  91.1 1.4 copy-start.18
  92.5 1.3 copy-start.20
  93.7 1.3 copy-start.22
  95.0 1.1 copy-start.24
  96.2 20.6 %copy-start.26 = (bf16[3,3,3,32,32]{4,3,2,1,0:T(8,128)(2,1)S(1)}, bf16[3,3,3,32,32]{4,3,2,1,0:T(8,128)(2,1)}, u32[]{:S(2)}) copy-start(bf16[3,3,3,32,32]{4,3,2,1,0:T(8,128)(2,1)} %param.14) | copy-start | bytes 165892
  108.1 39.0 %copy-start.25 = (bf16[10,32,1280]{2,1,0:T(8,128)(2,1)S(1)}, bf16[10,32,1280]{2,1,0:T(8,128)(2,1)}, u32[]{:S(2)}) copy-start(bf16[10,32,1280]{2,1,0:T(8,128)(2,1)} %copy-done.23) | copy-start | bytes 2457604
  108.1 17.0 %all-to-all-start.2 = ((bf16[32,32,128]{2,1,0:T(8,128)(2,1)}), bf16[32,32,128]{2,1,0:T(8,128)(2,1)S(1)}, u32[]{:S(2)}, u32[]{:S(2)}) async-start(bf16[32,32,128]{2,1,0:T(8,128)(2,1)} %get-tuple-element.51), calls=%async_computation.2 | async-start | bytes 524288 | tf_op jit(solution)/shard_map/all_to_all | solution.py:422
  125.8 14.2 %all-to-all-start.3 = ((bf16[8,32,128]{2,1,0:T(8,128)(2,1)}), bf16[8,32,128]{2,1,0:T(8,128)(2,1)S(1)}, u32[]{:S(2)}, u32[]{:S(2)}) async-start(bf16[8,32,128]{2,1,0:T(8,128)(2,1)} %shard_map.159), calls=%async_computation.3 | async-start | bytes 131072 | tf_op jit(solution)/shard_map/all_to_all | solution.py:422
  141.0 14.2 %all-to-all-start.4 = ((bf16[32,24,128]{2,1,0:T(8,128)(2,1)}), bf16[32,24,128]{2,1,0:T(8,128)(2,1)S(1)}, u32[]{:S(2)}, u32[]{:S(2)}) async-start(bf16[32,24,128]{2,1,0:T(8,128)(2,1)} %get-tuple-element.55), calls=%async_computation.4 | async-start | bytes 393216 | tf_op jit(solution)/shard_map/all_to_all | solution.py:422
  (12 other events, 11.6 us)
where the time goes:
time: 158 us; the launch traced here: 156 us
  starting transfers between devices  78.7 us (50%)
  Pallas kernels  30 us (19%)
  local copies, waits for them, and re-layouts  26.4 us (17%)
  waiting for transfers between devices  20.1 us (13%)
    all_to_all x5, starting transfers between devices, exchanged(): return lax.all_to_all(array, axes, 0, 0, tiled=True)  61.3 us
    unnamed x62, local copies, waits for them, and re-layouts  23.6 us
    all_to_all x5, waiting for transfers between devices, exchanged(): return lax.all_to_all(array, axes, 0, 0, tiled=True)  18.1 us
    ppermute x8, starting transfers between devices, per_device(): received.append(lax.ppermute(message, ('sx', 'sy'), pairs))  17.3 us
    pallas_call x1, Pallas kernels, per_device(): call(middle_kernel, [shaped((32, 32, 128), BF16), shaped((B + 2, C, (B +...  12 us
    pallas_call x1, Pallas kernels, per_device(): pl.pallas_call(last_kernel, out_shape=shaped((1, C, B, B, Z), BF16), in_s...  4 us
    pallas_call x1, Pallas kernels, per_device(): call(extend_kernel, [shaped((B + 2, C, (B + 2) * Z), BF16), shaped((B + 4...  3.84 us
    pallas_call x1, Pallas kernels, per_device(): call(spread_kernel, [block, block, block, shaped((B, 3 * C, B * Z), BF16)...  3.39 us
  transfers between devices with their start and end apart: 13, of which 4 were waited for; matrix products, arithmetic and copies ran while one was open for 2% of the time, Pallas kernels for 9%

commit v1 on v0

v1 whole, which is shorter than its diff:
```python
import math

import jax
import jax.numpy as jnp
from jax import lax
from jax.experimental import pallas as pl
from jax.experimental.pallas import tpu as pltpu
from jax.sharding import Mesh
from jax.sharding import PartitionSpec as P

DP = ("dp_0", "dp_1")
ALL = ("dp_0", "dp_1", "sx", "sy")
PLANE = ("dp_1", "sx", "sy")
EPS = 1e-05
F32 = jnp.float32
BF16 = jnp.bfloat16
C = 32
B = 8
Z = 128
CELLS = float(16 * 32 * 32 * Z)
SCALE = 1.0 / math.sqrt(CELLS)

VMEM = pltpu.MemorySpace.VMEM
SMEM = pltpu.MemorySpace.SMEM
HBM = pltpu.MemorySpace.HBM
FIELDS = (("c2", 2), ("ug", 2), ("c1", 1))


def span(side, width):
    return range(B - width, B) if side > 0 else range(width)


def landing(side, width):
    return range(B + width, B + 2 * width) if side > 0 else range(width)


def layers_x(side):
    return [(f, x) for f, w in FIELDS for x in span(side, w)]


def places_x(side):
    return [(f, x) for f, w in FIELDS for x in landing(side, w)]


def slabs_y(side):
    return [(f, y, x) for f, w in FIELDS for y in span(side, w) for x in range(B + 2 * w)]


def places_y(side):
    runs, first = [], 0
    for f, w in FIELDS:
        for y in landing(side, w):
            runs.append((first, B + 2 * w, f, y))
            first += B + 2 * w
    return runs


def call(kernel, outs, scratch=(), flops=0, spaces=(), limit=6, homes=None):
    single = not isinstance(outs, (list, tuple))
    shapes = [outs] if single else list(outs)
    homes = homes or [VMEM] * len(shapes)
    specs = [pl.BlockSpec(memory_space=space) for space in homes]
    shapes = [HBM(x.shape, x.dtype) if home == HBM else x for x, home in zip(shapes, homes)]
    f = pl.pallas_call(
        kernel,
        out_shape=shapes[0] if single else tuple(shapes),
        in_specs=[pl.BlockSpec(memory_space=space) for space in spaces],
        out_specs=specs[0] if single else tuple(specs),
        scratch_shapes=list(scratch),
        compiler_params=pltpu.CompilerParams(vmem_limit_bytes=limit * 2**20),
        cost_estimate=pl.CostEstimate(flops=flops, bytes_accessed=1 << 20, transcendentals=0),
    )

    def placed(*arguments):
        return f(
            *[
                pltpu.with_memory_space_constraint(x, HBM) if space == HBM else x
                for x, space in zip(arguments, spaces)
            ]
        )

    return placed


def started(pairs, sems):
    copies = [pltpu.make_async_copy(src, dst, sems.at[n]) for n, (src, dst) in enumerate(pairs)]
    for copy in copies:
        copy.start()
    return copies


def shaped(dims, kind):
    return jax.ShapeDtypeStruct(dims, kind)


def across(columns):
    return jnp.sum(jnp.transpose(columns), axis=0, keepdims=True)


def down(row):
    return jnp.transpose(jnp.broadcast_to(row, (128, 128)))


def arrived(ref):
    total = jnp.sum(ref[...].reshape(ref.shape[0], 128), axis=0, keepdims=True)
    return total


def shifted(slab, lane):
    before = jnp.where(lane == 0, 0.0, pltpu.roll(slab, 1, axis=1))
    after = jnp.where(lane == Z - 1, 0.0, pltpu.roll(slab, Z - 1, axis=1))
    return jnp.concatenate([before, slab, after], 0)


def lanes():
    return lax.broadcasted_iota(jnp.int32, (C, Z), 1)


def spread_kernel(
    one_ref, two_ref, up_ref, vol_ref, c1_ref, c2_ref, ug_ref, vol3_out, down_ref, up_x_ref, stat_ref,
    held, tmp, vol3, sems, out_sem,
):
    sources = (("vol", vol_ref, None), ("c1", one_ref, c1_ref), ("c2", two_ref, c2_ref), ("ug", up_ref, ug_ref))
    copies = started([(src.at[0], held.at[n]) for n, (_, src, _) in enumerate(sources)], sems)
    lane = lanes()
    parts = []
    for n, (name, _, dst) in enumerate(sources):
        copies[n].wait()
        tmp[...] = held[n].reshape(C * B * B, Z).astype(F32)
        total, squares = jnp.zeros((C, Z), F32), jnp.zeros((C, Z), F32)
        for x in range(B):
            for y in range(B):
                slab = tmp[pl.ds(x * B + y, C, stride=B * B), :]
                if name == "vol":
                    vol3[x, :, y * Z : (y + 1) * Z] = shifted(slab, lane).astype(BF16)
                    continue
                if name in ("c1", "c2"):
                    total, squares = total + slab, squares + slab * slab
                dst[x, :, y * Z : (y + 1) * Z] = slab.astype(BF16)
        if name == "vol":
            leaving = pltpu.make_async_copy(vol3, vol3_out, out_sem.at[0])
            leaving.start()
        if name in ("c1", "c2"):
            parts += [total, squares]
    own = {"c1": c1_ref, "c2": c2_ref, "ug": ug_ref}
    for side, ref in ((-1, down_ref), (1, up_x_ref)):
        for i, (f, x) in enumerate(layers_x(side)):
            ref[i] = own[f][x]
    row = across(jnp.concatenate(parts, 0))
    stat_ref[...] = jnp.broadcast_to(row[None], stat_ref.shape)
    leaving.wait()


def pack_kernel(c1_ref, c2_ref, ug_ref, low_ref, high_ref, down_ref, up_ref):
    where = {}
    for f, w, ref in (("c1", 1, c1_ref), ("c2", 2, c2_ref), ("ug", 2, ug_ref)):
        for x in range(B):
            where[(f, x + w)] = (ref, x)
    for side, ref in ((-1, low_ref), (1, high_ref)):
        for i, key in enumerate(places_x(side)):
            where[key] = (ref, i)
    for side, out in ((-1, down_ref), (1, up_ref)):
        for i, (f, y, x) in enumerate(slabs_y(side)):
            ref, n = where[(f, x)]
            out[i] = ref[n, :, y * Z : (y + 1) * Z]


def extend_kernel(
    pos_ref, stat_ref, par_ref, c1_ref, c2_ref, slope_ref, xlow_ref, xhigh_ref, vol3_in, ylow_in, yhigh_in,
    c1x_out, c2x_out, slopex_out, turn_out, act3_out, r_ref, c1x, c2x, slopex, turn, act3, ugx, vol3, sems, out_sems,
):
    target = {"c1": c1x, "c2": c2x, "ug": ugx}
    pairs = []
    for side, ref in ((-1, ylow_in), (1, yhigh_in)):
        for first, count, f, y in places_y(side):
            pairs.append((ref.at[pl.ds(first, count)], target[f].at[:, :, pl.ds(y * Z, Z)]))
    pairs.append((vol3_in, vol3))
    arriving = started(pairs, sems)
    (mean1, inv1), (mean2, inv2) = norms(stat_ref)
    gain1, bias1, gain2, bias2 = par_ref[0:32], par_ref[32:64], par_ref[64:96], par_ref[96:128]
    lane = lanes()

    def activation(x, carry):
        for y in range(B):
            cut = slice(y * Z, (y + 1) * Z)
            cent = (c1_ref[x, :, cut].astype(F32) - mean1) * inv1
            pre = gain1 * cent + bias1
            s = sigmoid(pre)
            act3[x, :, cut] = shifted((pre * s).astype(BF16).astype(F32), lane).astype(BF16)
            turn[x + 1, :, (y + 1) * Z : (y + 2) * Z] = s * (1.0 + pre * (1.0 - s))
        return carry

    lax.fori_loop(0, B, activation, 0)
    leaving = started([(act3, act3_out)], out_sems)
    for f, w, own in (("c1", 1, c1_ref), ("c2", 2, c2_ref)):
        for x in range(B):
            target[f][x + w, :, w * Z : (w + B) * Z] = own[x]
    width = dict(FIELDS)
    for side, ref in ((-1, xlow_ref), (1, xhigh_ref)):
        for i, (f, x) in enumerate(places_x(side)):
            w = width[f]
            target[f][x, :, w * Z : (w + B) * Z] = ref[i]
    for copy in arriving:
        copy.wait()
    leaving += started([(c1x, c1x_out), (c2x, c2x_out)], out_sems.at[pl.ds(1, 2)])

    def slope_at(x, y):
        cut = slice(y * Z, (y + 1) * Z)
        cent = (c2x[x, :, cut].astype(F32) - mean2) * inv2
        slopex[x, :, cut] = ugx[x, :, cut].astype(F32) * silu_slope(gain2 * cent + bias2)

    def ends(i, carry):
        x = jnp.where(i < 2, i, i + B)
        for y in range(B + 4):
            slope_at(x, y)
        return carry

    lax.fori_loop(0, 4, ends, 0)

    def between(x, carry):
        for y in (0, 1, B + 2, B + 3):
            slope_at(x + 2, y)
        slopex[x + 2, :, 2 * Z : (2 + B) * Z] = slope_ref[x]
        return carry

    lax.fori_loop(0, B, between, 0)
    leaving += started([(slopex, slopex_out)], out_sems.at[pl.ds(3, 1)])

    def turn_at(x, y):
        cut = slice(y * Z, (y + 1) * Z)
        cent = (c1x[x, :, cut].astype(F32) - mean1) * inv1
        turn[x, :, cut] = silu_slope(gain1 * cent + bias1)

    for x in (0, B + 1):
        for y in range(B + 2):
            turn_at(x, y)

    def sides(x, carry):
        turn_at(x + 1, 0)
        turn_at(x + 1, B + 1)
        return carry

    lax.fori_loop(0, B, sides, 0)
    leaving += started([(turn, turn_out)], out_sems.at[pl.ds(4, 1)])

    sx, sy = pos_ref[0], pos_ref[1]
    row = lax.broadcasted_iota(jnp.int32, (16, B * Z), 0)
    gy = sy * B + lax.broadcasted_iota(jnp.int32, (16, B * Z), 1) // Z
    wy = gy + 1 - row % 3
    ok_y = (wy >= 0) & (wy < 4 * B) & (row < 9)

    def body(x, acc):
        wx = sx * B + x + 1 - row // 3
        inside = jnp.where(ok_y & (wx >= 0) & (wx < 4 * B), 1.0, 0.0).astype(BF16)
        lhs = jnp.concatenate([windows(c1x, x, 2, 2, B), inside], 0)
        return acc + lax.dot_general(lhs, vol3[x], TRANSPOSED, preferred_element_type=F32)

    acc = lax.fori_loop(0, B, body, jnp.zeros((9 * C + 16, 3 * C), F32))
    r_ref[...] = turned(acc).astype(BF16)
    for copy in leaving:
        copy.wait()


TRANSPOSED = (((1,), (1,)), ((), ()))


def turned(acc):
    rows = acc.shape[0]
    full = jnp.concatenate([acc, jnp.zeros((384 - rows, 3 * C), F32)], 0)
    full = jnp.concatenate([full, jnp.zeros((384, 128 - 3 * C), F32)], 1)
    return jnp.concatenate([jnp.transpose(full[i * 128 : (i + 1) * 128]) for i in range(3)], 1)


def moments(total, squares):
    mean = total * (1.0 / CELLS)
    inv = lax.rsqrt(squares * (1.0 / CELLS) - mean * mean + EPS)
    return mean, inv


def norms(stat_ref):
    cols = down(stat_ref[0:1])
    return moments(cols[0:32], cols[32:64]), moments(cols[64:96], cols[96:128])


def sigmoid(v):
    return 0.5 * jnp.tanh(0.5 * v) + 0.5


def silu_slope(v):
    s = sigmoid(v)
    return s * (1.0 + v * (1.0 - s))


def sums_two_kernel(got_ref, par_ref, c2_ref, ug_ref, out_ref, row_ref, slope_ref):
    row = arrived(got_ref)
    row_ref[...] = jnp.broadcast_to(row, (8, 128))
    _, (mean2, inv2) = norms(row_ref)
    gain, bias = par_ref[64:96], par_ref[96:128]

    def body(x, acc):
        b, g = acc
        for y in range(B):
            cent = (c2_ref[x, :, y * Z : (y + 1) * Z].astype(F32) - mean2) * inv2
            up = ug_ref[x, :, y * Z : (y + 1) * Z].astype(F32)
            slope = up * silu_slope(gain * cent + bias)
            slope_ref[x, :, y * Z : (y + 1) * Z] = slope
            b, g = b + slope, g + slope * cent
        return b, g

    zero = jnp.zeros((C, Z), F32)
    b, g = lax.fori_loop(0, B, body, (zero, zero))
    out = across(jnp.concatenate([b, g, zero, zero], 0))
    out_ref[...] = jnp.broadcast_to(out[None], out_ref.shape)


def windows(ref, x, first, y_first, count):
    parts = []
    for kx in range(3):
        for ky in range(3):
            parts.append(ref[x + first - kx, :, (y_first - ky) * Z : (y_first - ky + count) * Z])
    return jnp.concatenate(parts, 0)


def unshift(t, y, lane):
    left = t[0:C, y * Z : (y + 1) * Z]
    mid = t[C : 2 * C, y * Z : (y + 1) * Z]
    right = t[2 * C : 3 * C, y * Z : (y + 1) * Z]
    out = mid + jnp.where(lane == Z - 1, 0.0, pltpu.roll(left, Z - 1, axis=1))
    return out + jnp.where(lane == 0, 0.0, pltpu.roll(right, 1, axis=1))


def as_matrix(src, dst):
    for kz in range(3):
        parts = [src[kx, ky, kz].astype(F32) for kx in range(3) for ky in range(3)]
        dst[kz * C : (kz + 1) * C, :] = jnp.concatenate(parts, 1).astype(BF16)


def three(value):
    hi = value.astype(BF16).astype(F32)
    mid = (value - hi).astype(BF16).astype(F32)
    lo = value - hi - mid
    return hi, mid, lo


def middle_kernel(
    pos_ref, got_ref, stat_ref, par_ref, w_in, c1x_in, c2x_in, slopex_in, turn_in, vol3_in, act3_in, r_in,
    msg_ref, slope_ref, row_ref, w_ref, c1x_ref, c2x_ref, slopex_ref, turn_ref, vol3_ref, act3_ref, r_ref,
    raw, grad, msg, sems,
):
    arriving = started(
        [
            (slopex_in, slopex_ref),
            (c2x_in, c2x_ref),
            (w_in, raw),
            (turn_in, turn_ref),
            (c1x_in, c1x_ref),
            (vol3_in, vol3_ref),
            (act3_in, act3_ref),
            (r_in, r_ref),
        ],
        sems,
    )
    sx, sy = pos_ref[0], pos_ref[1]
    row = arrived(got_ref)
    row_ref[...] = jnp.broadcast_to(row, (8, 128))
    cols = down(row)
    (mean1, inv1), (mean2, inv2) = norms(stat_ref)
    amp = par_ref[64:96] * inv2
    by = amp * inv2 * cols[32:64] * (1.0 / CELLS)
    off = amp * cols[0:32] * (1.0 / CELLS) - by * mean2
    lane = lanes()
    inside_y = {
        y: jnp.where(sy > 0, 1.0, 0.0) if y < 2 else jnp.where(sy < 3, 1.0, 0.0)
        for y in (0, 1, B + 2, B + 3)
    }

    def first(x, carry):
        gx = sx * B + x - 2
        inside_x = jnp.where((gx >= 0) & (gx < 4 * B), 1.0, 0.0)
        for y in range(B + 4):
            cut = slice(y * Z, (y + 1) * Z)
            value = amp * slopex_ref[x, :, cut] - by * c2x_ref[x, :, cut].astype(F32) - off
            keep = inside_x * inside_y[y] if y in inside_y else inside_x
            grad[x, :, cut] = (value * keep).astype(BF16)
        return carry

    arriving[0].wait()
    arriving[1].wait()
    lax.fori_loop(0, B + 4, first, 0)
    arriving[2].wait()
    as_matrix(raw, w_ref)
    arriving[3].wait()
    arriving[4].wait()
    inside_y = {0: jnp.where(sy > 0, 1.0, 0.0), B + 1: jnp.where(sy < 3, 1.0, 0.0)}

    def second(x, acc):
        b, g = acc
        gx = sx * B + x - 1
        inside_x = jnp.where((gx >= 0) & (gx < 4 * B), 1.0, 0.0)
        own_x = jnp.where((x >= 1) & (x <= B), 1.0, 0.0)
        t = jnp.dot(w_ref[...], windows(grad, x, 2, 2, B + 2), preferred_element_type=F32)
        bx, gsum = jnp.zeros((C, Z), F32), jnp.zeros((C, Z), F32)
        for y in range(B + 2):
            cut = slice(y * Z, (y + 1) * Z)
            slope = unshift(t, y, lane) * turn_ref[x, :, cut]
            if 1 <= y <= B:
                bx, gsum = bx + slope, gsum + slope * c1x_ref[x, :, cut].astype(F32)
            inside = inside_x * inside_y[y] if y in inside_y else inside_x
            slope_ref[x, :, cut] = (slope * inside).astype(BF16)
        gsum = (gsum - mean1 * bx) * inv1
        return b + bx * own_x, g + gsum * own_x

    zero = jnp.zeros((C, Z), F32)
    b, g = lax.fori_loop(0, B + 2, second, (zero, zero))

    def third(x, acc):
        s, f = acc
        s = s + lax.dot_general(windows(slope_ref, x, 2, 2, B), vol3_ref[x], TRANSPOSED, preferred_element_type=F32)
        f = f + lax.dot_general(windows(grad, x, 3, 3, B), act3_ref[x], TRANSPOSED, preferred_element_type=F32)
        return s, f

    for copy in arriving[5:]:
        copy.wait()
    empty = jnp.zeros((9 * C, 3 * C), F32)
    s, f = lax.fori_loop(0, B, third, (empty, empty))
    sums = across(jnp.concatenate([b, g, zero, zero], 0))
    hi, mid, lo = three(sums)
    for m, part in enumerate((turned(s), r_ref[...].astype(F32), turned(f))):
        for kz in range(3):
            for t in range(3):
                msg[:, m * 9 + kz * 3 + t, :] = part[kz * C : (kz + 1) * C, t * 128 : (t + 1) * 128]
    for i, part in enumerate((hi, mid, lo)):
        msg[:, 27 + i, :] = jnp.broadcast_to(part, (C, 128))
    msg[:, 30, :] = zero
    msg[:, 31, :] = zero
    msg_ref[...] = msg[...].astype(BF16)


def relay_kernel(got_ref, out_ref):
    total = jnp.sum(got_ref[...].astype(F32), axis=0)
    sums = total[27:28] + total[28:29] + total[29:30]
    hi, mid, lo = three(sums)
    out = jnp.concatenate([total[0:27], hi, mid, lo, total[30:32]], 0).astype(BF16)
    out_ref[...] = jnp.broadcast_to(out[None], out_ref.shape)


def share_kernel(got_ref, stat_ref, lanepar_ref, out_ref, row_ref):
    total = jnp.sum(got_ref[...].astype(F32), axis=0)
    sums = total[27:28] + total[28:29] + total[29:30]
    row_ref[...] = jnp.broadcast_to(sums, (8, 128))
    lane = lax.broadcasted_iota(jnp.int32, (1, 128), 1)
    stat = stat_ref[0:1]
    mean = stat * (1.0 / CELLS)
    squares = pltpu.roll(stat, 96, axis=1) * (1.0 / CELLS)
    inv = lax.rsqrt(jnp.where(lane < C, squares - mean * mean, 0.0) + EPS)
    g = pltpu.roll(sums, 96, axis=1)
    alpha = lanepar_ref[0:1] * inv
    gamma = alpha * inv * g * (1.0 / CELLS)
    delta = alpha * sums * (1.0 / CELLS) - gamma * mean
    rows = jnp.where(lane < C, jnp.concatenate([alpha, gamma, delta], 0), 0.0)
    rows = jnp.concatenate([rows, jnp.zeros((5, 128), F32)], 0)
    a = lax.broadcasted_iota(jnp.int32, (128, 384), 0)
    o = lax.broadcasted_iota(jnp.int32, (128, 384), 1)
    tile = jnp.where(o % C == a, 1.0, 0.0)
    wide = jnp.dot(rows, tile, precision=lax.Precision.HIGHEST, preferred_element_type=F32)
    spread = jnp.where((o // C + C == a) & (o < 9 * C), 1.0, 0.0)
    marks = jnp.concatenate([total[11:12], total[14:15], total[17:18], jnp.zeros((5, 128), F32)], 0)
    ones = jnp.dot(marks, spread, precision=lax.Precision.HIGHEST, preferred_element_type=F32)
    parts = []
    for kz in range(3):
        for t in range(3):
            cut = slice(t * 128, (t + 1) * 128)
            one = (
                wide[0:1, cut] * total[kz * 3 + t : kz * 3 + t + 1]
                - wide[1:2, cut] * total[9 + kz * 3 + t : 10 + kz * 3 + t]
                - wide[2:3, cut] * ones[kz : kz + 1, cut]
            )
            parts.append(one)
    out = jnp.concatenate(parts + [total[18:27], jnp.zeros((6, 128), F32)], 0) * SCALE
    out_ref[...] = jnp.broadcast_to(out.astype(BF16)[None], out_ref.shape)


def last_kernel(
    mask_ref, sum_ref, two_ref, stat_ref, par_ref, slope_ref, w_in, c1x_in,
    out_ref, gain1_ref, bias1_ref, gain2_ref, bias2_ref, grad, tmp, w_ref, raw, c1x_ref, sems,
):
    arriving = started([(w_in, raw), (c1x_in, c1x_ref)], sems)
    for ref, bias_ref, gain_ref in ((sum_ref, bias1_ref, gain1_ref), (two_ref, bias2_ref, gain2_ref)):
        scaled = ref[0:1] * SCALE
        bias_ref[...] = scaled[:, 0:C]
        gain_ref[...] = pltpu.roll(scaled, 96, axis=1)[:, 0:C]
    cols = down(sum_ref[0:1])
    (mean, inv), _ = norms(stat_ref)
    b, g = cols[0:32] * (1.0 / CELLS), cols[32:64] * (1.0 / CELLS)
    amp = par_ref[0:32] * inv
    by = amp * inv * g
    off = amp * b - by * mean
    lane = lanes()
    sx, sy = mask_ref[0], mask_ref[1]
    inside_y = {0: jnp.where(sy > 0, 1.0, 0.0), B + 1: jnp.where(sy < 3, 1.0, 0.0)}

    def first(x, carry):
        gx = sx * B + x - 1
        inside_x = jnp.where((gx >= 0) & (gx < 4 * B), 1.0, 0.0)
        for y in range(B + 2):
            cut = slice(y * Z, (y + 1) * Z)
            value = amp * slope_ref[x, :, cut].astype(F32) - by * c1x_ref[x, :, cut].astype(F32) - off
            keep = inside_x * inside_y[y] if y in inside_y else inside_x
            grad[x, :, cut] = (value * keep).astype(BF16)
        return carry

    for copy in arriving:
        copy.wait()
    as_matrix(raw, w_ref)
    lax.fori_loop(0, B + 2, first, 0)

    for x in range(B):
        t = jnp.dot(w_ref[...], windows(grad, x, 2, 2, B), preferred_element_type=F32)
        for y in range(B):
            tmp[pl.ds(x * B + y, C, stride=B * B), :] = unshift(t, y, lane)
    out_ref[0] = tmp[...].astype(BF16).reshape(C, B, B, Z)


def filters_kernel(got_ref, one_ref, two_ref, tmp):
    tmp[...] = got_ref[...].astype(F32)
    for m, ref in enumerate((one_ref, two_ref)):
        for kz in range(3):
            for t in range(3):
                slab = tmp[:, m * 9 + kz * 3 + t, :]
                for i in range(4):
                    k = 4 * t + i
                    if k < 9:
                        ref[k // 3, k % 3, kz] = slab[:, i * C : (i + 1) * C]


def exchanged(array, axes):
    return lax.all_to_all(array, axes, 0, 0, tiled=True)


def per_device(
    volume, conv_one, conv_two, upper_grad, weight_one, weight_two, gain_one, bias_one, gain_two, bias_two
):
    pos = jnp.stack([lax.axis_index("sx"), lax.axis_index("sy")]).astype(jnp.int32)
    packed = jnp.concatenate([gain_one, bias_one, gain_two, bias_two])
    par = jnp.broadcast_to(packed[:, None], (128, 128))
    lanepar = jnp.broadcast_to(packed[None, :], (8, 128))
    everyone = shaped((256, 1, 128), F32)
    block = shaped((B, C, B * Z), BF16)
    three_fold = shaped((B, 3 * C, B * Z), BF16)
    near = shaped((B + 2, C, (B + 2) * Z), BF16)
    far = shaped((B + 4, C, (B + 4) * Z), BF16)
    weights = shaped((3, 3, 3, C, C), BF16)
    near_wide, far_wide, block_wide = (shaped(a.shape, F32) for a in (near, far, block))
    row = shaped((8, 128), F32)

    def room(like):
        return pltpu.VMEM(like.shape, like.dtype)

    def sems(count):
        return pltpu.SemaphoreType.DMA((count,))

    along_x = shaped((len(layers_x(1)), C, B * Z), BF16)
    c1, c2, ug, vol3, send_down, send_up, stats = call(
        spread_kernel,
        [block, block, block, three_fold, along_x, along_x, everyone],
        scratch=[
            pltpu.VMEM((4, C, B, B, Z), BF16),
            pltpu.VMEM((C * B * B, Z), F32),
            room(three_fold),
            sems(4),
            sems(1),
        ],
        spaces=[HBM] * 4,
        homes=[VMEM] * 3 + [HBM] + [VMEM] * 3,
        limit=10,
    )(conv_one, conv_two, upper_grad, volume)
    up = [(i, i + 1) for i in range(3)]
    down_ = [(i + 1, i) for i in range(3)]
    x_low = lax.ppermute(send_up, "sx", up)
    x_high = lax.ppermute(send_down, "sx", down_)
    got_stats = exchanged(stats, ALL)
    along_y = shaped((len(slabs_y(1)), C, Z), BF16)
    send_down, send_up = call(pack_kernel, [along_y, along_y], spaces=[VMEM] * 5)(c1, c2, ug, x_low, x_high)
    y_low = lax.ppermute(send_up, "sy", up)
    y_high = lax.ppermute(send_down, "sy", down_)

    sums_two, stat_row, slope_two = call(
        sums_two_kernel, [everyone, row, block_wide], spaces=[VMEM] * 4
    )(got_stats, par, c2, ug)
    got_two = exchanged(sums_two, ALL)
    r_shape = shaped((128, 384), BF16)
    c1x, c2x, slopex, turn, act3, r = call(
        extend_kernel,
        [near, far, far_wide, near_wide, three_fold, r_shape],
        scratch=[
            room(near), room(far), room(far_wide), room(near_wide), room(three_fold), room(far), room(three_fold), sems(11), sems(5)
        ],
        flops=5 * 10**9,
        spaces=[SMEM] + [VMEM] * 7 + [HBM] * 3,
        homes=[HBM] * 5 + [VMEM],
        limit=16,
    )(pos, stat_row, par, c1, c2, slope_two, x_low, x_high, vol3, y_low, y_high)

    terms, slope, row_two = call(
        middle_kernel,
        [shaped((32, 32, 128), BF16), near, row],
        scratch=[
            pltpu.VMEM((3 * C, 9 * C), BF16), room(near), room(far), room(far_wide), room(near_wide), room(three_fold),
            room(three_fold), room(r_shape), room(weights), room(far), pltpu.VMEM((32, 32, 128), F32), sems(8),
        ],
        flops=4 * 10**9,
        spaces=[SMEM] + [VMEM] * 3 + [HBM] * 8,
        limit=18,
    )(pos, got_two, stat_row, par, weight_two, c1x, c2x, slopex, turn, vol3, act3, r)

    got_terms = exchanged(terms, PLANE)
    relay = call(relay_kernel, shaped((8, 32, 128), BF16), spaces=[VMEM])(got_terms)
    got_relay = exchanged(relay, "dp_0")
    shares, row_one = call(
        share_kernel, [shaped((32, 24, 128), BF16), row], spaces=[VMEM] * 3
    )(got_relay, stat_row, lanepar)
    got_shares = exchanged(shares, PLANE)
    vector = shaped((1, C), F32)
    input_grad, gain_one_grad, bias_one_grad, gain_two_grad, bias_two_grad = call(
        last_kernel,
        [shaped((1, C, B, B, Z), BF16), vector, vector, vector, vector],
        scratch=[
            room(near), pltpu.VMEM((C * B * B, Z), F32), pltpu.VMEM((3 * C, 9 * C), BF16), room(weights), room(near), sems(2)
        ],
        flops=4 * 10**9,
        spaces=[SMEM] + [VMEM] * 5 + [HBM] * 2,
        limit=10,
    )(pos, row_one, row_two, stat_row, par, slope, weight_one, c1x)
    filters = shaped((3, 3, 3, C, C), F32)
    filter_one, filter_two = call(
        filters_kernel, [filters, filters], scratch=[pltpu.VMEM((32, 24, 128), F32)], spaces=[VMEM]
    )(got_shares)
    return (
        input_grad, filter_one, filter_two, gain_one_grad[0], bias_one_grad[0], gain_two_grad[0], bias_two_grad[0]
    )


def solution(mesh):
    finer = Mesh(
        mesh.devices.reshape(8, 2, mesh.shape["sx"], mesh.shape["sy"]), ("dp_0", "dp_1", "sx", "sy")
    )
    field = P(DP, None, "sx", "sy", None)
    return jax.shard_map(
        per_device,
        mesh=finer,
        in_specs=(field,) * 4 + (P(),) * 6,
        out_specs=(field,) + (P(),) * 6,
        check_vma=False,
    )
```

time: 158 us -> 129 us (0.82)
  starting transfers between devices: 78.7 us -> 39 us
  local copies, waits for them, and re-layouts: 26.4 us -> 0.73 us
  blocking collectives: 0 us -> 24.1 us
  waiting for transfers between devices: 20.1 us -> 30.6 us
  Pallas kernels: 30 us -> 33 us
    all_to_all x5 -> x3, starting transfers between devices: 61.3 us -> 28.4 us  [exchanged(): return lax.all_to_all(array, axes, 0, 0, tiled=True)]
    all_to_all x0 -> x2, blocking collectives: none -> 24.1 us  [exchanged(): return lax.all_to_all(array, axes, 0, 0, tiled=True)]
    unnamed x62 -> x10, local copies, waits for them, and re-layouts: 23.6 us -> 0.66 us
    ppermute x8 -> x4, waiting for transfers between devices: 1.98 us -> 8.91 us  [the longest x1 5.06 us: per_device(): x_low = lax.ppermute(send_up, 'sx', up)]
    ppermute x8 -> x4, starting transfers between devices: 17.3 us -> 10.6 us  [the longest x1 4.17 us: per_device(): x_low = lax.ppermute(send_up, 'sx', up)]
    all_to_all x5 -> x3, waiting for transfers between devices: 18.1 us -> 21.7 us  [exchanged(): return lax.all_to_all(array, axes, 0, 0, tiled=True)]
    pallas_call x10 -> x9, Pallas kernels: 30 us -> 33 us  [placed(): f(*[pltpu.with_memory_space_constraint(x, HBM) if space == HBM else x for...]
  transfers between devices with their start and end apart: 13 -> 7, of which waited for: 4 -> 5; matrix products, arithmetic and copies ran while one was open for 2% -> 0% of each run, Pallas kernels for 9% -> 10%
where the time goes in v1:
time: 129 us
  starting transfers between devices  39 us (30%)
  Pallas kernels  33 us (26%)
  waiting for transfers between devices  30.6 us (24%)
  blocking collectives  24.1 us (19%)
    pallas_call x9, Pallas kernels, placed(): f(*[pltpu.with_memory_space_constraint(x, HBM) if space == HBM else x for...  33 us
    all_to_all x3, starting transfers between devices, exchanged(): return lax.all_to_all(array, axes, 0, 0, tiled=True)  28.4 us
    all_to_all x2, blocking collectives, exchanged(): return lax.all_to_all(array, axes, 0, 0, tiled=True)  24.1 us
    all_to_all x3, waiting for transfers between devices, exchanged(): return lax.all_to_all(array, axes, 0, 0, tiled=True)  21.7 us
    ppermute x1, waiting for transfers between devices, per_device(): x_low = lax.ppermute(send_up, 'sx', up)  5.06 us
    ppermute x1, starting transfers between devices, per_device(): x_low = lax.ppermute(send_up, 'sx', up)  4.17 us
    ppermute x1, starting transfers between devices, per_device(): y_low = lax.ppermute(send_up, 'sy', up)  3.88 us
    ppermute x1, waiting for transfers between devices, per_device(): x_high = lax.ppermute(send_down, 'sx', down_)  3.85 us
  transfers between devices with their start and end apart: 7, of which 5 were waited for; matrix products, arithmetic and copies ran while one was open for 0% of the time, Pallas kernels for 10%

profile of v1, /device:TPU:1, one launch (start us, length us, event | category | flops | bytes accessed | tf_op | source)
XLA Modules:
  0.0 128.5 jit_solution(17278659549527246774)
XLA Ops:
  0.6 4.8 %shard_map.153 = (bf16[8,32,1024]{2,1,0:T(8,128)(2,1)S(1)}, bf16[8,32,1024]{2,1,0:T(8,128)(2,1)S(1)}, bf16[8,32,1024]{2,1,0:T(8,128)(2,1)S(1)}, bf16[8,96,1024]{...) custom-call(bf16[1,32,8,8,128]{4,3,2,1,0:T(8,128)(2,1)} %one_ref.1, ...), custom_call_target="tpu_custom_call" | custom-call | bytes 1048576 | tf_op jit(solution)/shard_map/pallas_call | solution.py:75
  5.4 0.0 copy-start.1
  5.4 0.0 copy-start.2
  5.4 0.0 copy-start.3
  5.5 0.0 copy-start.4
  5.5 4.2 %collective-permute-start = (bf16[5,32,1024]{2,1,0:T(8,128)(2,1)S(1)}, bf16[5,32,1024]{2,1,0:T(8,128)(2,1)S(1)}, u32[]{:S(2)}, u32[]{:S(2)}) collective-permute-start(bf16[5,32,1024]{2,1,0:T(8,128)(2,1)S(1)} %get-tuple-element.44), channel_id=1, source_target_pairs={{0,4},{4,8},{8,12},{1,5},{5,9},{9,13},{2,6},{6,10},{10,14},{3,7},{... | collective-permute-start | bytes 983048 | tf_op jit(solution)/shard_map/ppermute | solution.py:579
  9.6 1.3 %collective-permute-start.1 = (bf16[5,32,1024]{2,1,0:T(8,128)(2,1)S(1)}, bf16[5,32,1024]{2,1,0:T(8,128)(2,1)S(1)}, u32[]{:S(2)}, u32[]{:S(2)}) collective-permute-start(bf16[5,32,1024]{2,1,0:T(8,128)(2,1)S(1)} %get-tuple-element.45), channel_id=1, source_target_pairs={{4,0},{8,4},{12,8},{5,1},{9,5},{13,9},{6,2},{10,6},{14,10},{7,3},{... | collective-permute-start | bytes 983048 | tf_op jit(solution)/shard_map/ppermute | solution.py:580
  10.9 5.1 %collective-permute-done.low_ref.xlow_ref = bf16[5,32,1024]{2,1,0:T(8,128)(2,1)S(1)} collective-permute-done((bf16[5,32,1024]{2,1,0:T(8,128)(2,1)S(1)}, bf16[5,32,1024]{2,1,0:T(8,128)(2,1)S(1)}, u32[]{:S(2)}, u32[]{:S(2)}) %collective-permute-start) | collective-permute-done | bytes 327712 | tf_op jit(solution)/shard_map/ppermute | solution.py:579
  16.0 3.9 %collective-permute-done.1.high_ref.xhigh_ref = bf16[5,32,1024]{2,1,0:T(8,128)(2,1)S(1)} collective-permute-done((bf16[5,32,1024]{2,1,0:T(8,128)(2,1)S(1)}, bf16[5,32,1024]{2,1,0:T(8,128)(2,1)S(1)}, u32[]{:S(2)}, u32[]{:S(2)}) %collective-permute-start.1) | collective-permute-done | bytes 327712 | tf_op jit(solution)/shard_map/ppermute | solution.py:580
  19.9 1.1 shard_map.155
  21.0 3.9 %collective-permute-start.2 = (bf16[58,32,128]{2,1,0:T(8,128)(2,1)}, bf16[58,32,128]{2,1,0:T(8,128)(2,1)}, u32[]{:S(2)}, u32[]{:S(2)}) collective-permute-start(bf16[58,32,128]{2,1,0:T(8,128)(2,1)} %get-tuple-element.47), channel_id=1, source_target_pairs={{0,1},{1,2},{2,3},{4,5},{5,6},{6,7},{8,9},{9,10},{10,11},{12,13},{... | collective-permute-start | bytes 1425416 | tf_op jit(solution)/shard_map/ppermute | solution.py:584
  24.8 1.3 collective-permute-start.3
  26.1 16.8 %all-to-all-start = ((f32[256,1,128]{2,1,0:T(1,128)}), f32[256,1,128]{2,1,0:T(1,128)S(1)}, u32[]{:S(2)}, u32[]{:S(2)}) async-start(f32[256,1,128]{2,1,0:T(1,128)} %get-tuple-element.37), calls=%async_computation | async-start | bytes 262144 | tf_op jit(solution)/shard_map/all_to_all | solution.py:537
  43.0 0.1 pad_add_fusion.pos_ref.mask_ref
  43.1 0.1 pad_maximum_fusion
  43.2 12.8 %all-to-all-done.got_ref = f32[256,1,128]{2,1,0:T(1,128)S(1)} async-done(((f32[256,1,128]{2,1,0:T(1,128)}), f32[256,1,128]{2,1,0:T(1,128)S(1)}, u32[]{:S(2)}, u32[]{:S(2)}) %all-to-all-start) | async-done | bytes 131104 | tf_op jit(solution)/shard_map/all_to_all | solution.py:537
  56.0 0.1 broadcast_in_dim.4.par_ref
  56.1 1.8 %shard_map.154 = (f32[256,1,128]{2,1,0:T(1,128)}, f32[8,128]{1,0:T(8,128)S(1)}, f32[8,32,1024]{2,1,0:T(8,128)S(1)}) custom-call(f32[256,1,128]{2,1,0:T(1,128)S(1)} %all-to-all-done.got_ref, f32[128,128]{1,0:T(8,128)S(1)} %broadcast_in_dim.4.par_ref, bf16[8,32,1024]{2,1,0:T(8,128)(2,1)S(1)} %get-tuple-element.38.c2_ref, ...), custom_call_target="tpu_custom_call" | custom-call | bytes 1048576 | tf_op jit(solution)/shard_map/pallas_call | solution.py:75
  57.9 5.5 %all-to-all-start.1 = ((f32[256,1,128]{2,1,0:T(1,128)}), f32[256,1,128]{2,1,0:T(1,128)S(1)}, u32[]{:S(2)}, u32[]{:S(2)}) async-start(f32[256,1,128]{2,1,0:T(1,128)} %get-tuple-element.40), calls=%async_computation.1 | async-start | bytes 262144 | tf_op jit(solution)/shard_map/all_to_all | solution.py:537
  63.4 6.5 %shard_map.156 = (bf16[10,32,1280]{2,1,0:T(8,128)(2,1)}, bf16[12,32,1536]{2,1,0:T(8,128)(2,1)}, f32[12,32,1536]{2,1,0:T(8,128)}, f32[10,32,1280]{2,1,0:T(8,128)}...) custom-call(s32[2]{0:T(128)S(1)} %pad_add_fusion.pos_ref.mask_ref, f32[8,128]{1,0:T(8,128)S(1)} %get-tuple-element.41.stat_ref, ...), custom_call_target="tpu_custom_call" | custom-call | flops 5000000000 | bytes 1048576 | tf_op jit(solution)/shard_map/pallas_call | solution.py:75
  69.9 0.0 copy-start
  69.9 0.6 copy-done
  70.5 6.0 %all-to-all-done.1.got_ref = f32[256,1,128]{2,1,0:T(1,128)S(1)} async-done(((f32[256,1,128]{2,1,0:T(1,128)}), f32[256,1,128]{2,1,0:T(1,128)S(1)}, u32[]{:S(2)}, u32[]{:S(2)}) %all-to-all-start.1) | async-done | bytes 131104 | tf_op jit(solution)/shard_map/all_to_all | solution.py:537
  76.5 11.5 %shard_map.157 = (bf16[32,32,128]{2,1,0:T(8,128)(2,1)S(1)}, bf16[10,32,1280]{2,1,0:T(8,128)(2,1)S(1)}, f32[8,128]{1,0:T(8,128)S(1)}) custom-call(s32[2]{0:T(128)S(1)} %pad_add_fusion.pos_ref.mask_ref, f32[256,1,128]{2,1,0:T(1,128)S(1)} %all-to-all-done.1.got_ref, f32[8,128]{1,0:T(8,128)S(1)} %get-tuple-element.41.stat_ref, ...), custom_call_target="tpu_custom_call" | custom-call | flops 4000000000 | bytes 1048576 | tf_op jit(solution)/shard_map/pallas_call | solution.py:75
  88.0 11.8 %all_to_all.25.got_ref = bf16[32,32,128]{2,1,0:T(8,128)(2,1)S(1)} all-to-all(bf16[32,32,128]{2,1,0:T(8,128)(2,1)S(1)} %get-tuple-element.55), channel_id=1, replica_groups=mesh['dp_0'=8,'dp_1'=2,'sx'=4,'sy'=4] {'dp_1','sx','sy'}, dimensions={0} | all-to-all | bytes 524288 | tf_op jit(solution)/shard_map/all_to_all | solution.py:537
  99.8 0.1 shard_map.158
  99.9 12.3 %all_to_all.26.got_ref = bf16[8,32,128]{2,1,0:T(8,128)(2,1)S(1)} all-to-all(bf16[8,32,128]{2,1,0:T(8,128)(2,1)S(1)} %shard_map.158), channel_id=1, replica_groups=mesh['dp_0'=8,'dp_1'=2,'sx'=4,'sy'=4] {'dp_0'}, dimensions={0} | all-to-all | bytes 131072 | tf_op jit(solution)/shard_map/all_to_all | solution.py:537
  112.2 1.0 shard_map.159
  113.2 6.1 %all-to-all-start.4 = ((bf16[32,24,128]{2,1,0:T(8,128)(2,1)}), bf16[32,24,128]{2,1,0:T(8,128)(2,1)S(1)}, u32[]{:S(2)}, u32[]{:S(2)}) async-start(bf16[32,24,128]{2,1,0:T(8,128)(2,1)} %get-tuple-element.60), calls=%async_computation.4 | async-start | bytes 393216 | tf_op jit(solution)/shard_map/all_to_all | solution.py:537
  119.3 5.2 %shard_map.160 = (bf16[1,32,8,8,128]{4,3,2,1,0:T(8,128)(2,1)}, f32[1,32]{1,0:T(1,128)}, f32[1,32]{1,0:T(1,128)}, f32[1,32]{1,0:T(1,128)}, f32[1,32]{1,0:T(1,128)}) custom-call(s32[2]{0:T(128)S(1)} %pad_add_fusion.pos_ref.mask_ref, f32[8,128]{1,0:T(8,128)S(1)} %get-tuple-element.56.sum_ref, f32[8,128]{1,0:T(8,128)S(1)} %get-tuple-element.57.two_ref, ...), custom_call_target="tpu_custom_call" | custom-call | flops 4000000000 | bytes 1048576 | tf_op jit(solution)/shard_map/pallas_call | solution.py:75
  124.5 2.9 %all-to-all-done.4.got_ref = bf16[32,24,128]{2,1,0:T(8,128)(2,1)S(1)} async-done(((bf16[32,24,128]{2,1,0:T(8,128)(2,1)}), bf16[32,24,128]{2,1,0:T(8,128)(2,1)S(1)}, u32[]{:S(2)}, u32[]{:S(2)}) %all-to-all-start.4) | async-done | bytes 196640 | tf_op jit(solution)/shard_map/all_to_all | solution.py:537
  127.4 1.1 shard_map.161
  (7 shorter events, 0.0 us)
Async XLA Ops:
  5.4 37.7 %copy-start.1 = (f32[32]{0:T(128)S(1)}, f32[32]{0:T(128)}, u32[]{:S(2)}) copy-start(f32[32]{0:T(128)} %param.19) | copy-start | bytes 388
  5.4 37.6 %copy-start.2 = (f32[32]{0:T(128)S(1)}, f32[32]{0:T(128)}, u32[]{:S(2)}) copy-start(f32[32]{0:T(128)} %param.18) | copy-start | bytes 388
  5.4 37.6 %copy-start.3 = (f32[32]{0:T(128)S(1)}, f32[32]{0:T(128)}, u32[]{:S(2)}) copy-start(f32[32]{0:T(128)} %param.17) | copy-start | bytes 388
  5.5 37.6 %copy-start.4 = (f32[32]{0:T(128)S(1)}, f32[32]{0:T(128)}, u32[]{:S(2)}) copy-start(f32[32]{0:T(128)} %param.16) | copy-start | bytes 388
  5.5 10.5 %collective-permute-start = (bf16[5,32,1024]{2,1,0:T(8,128)(2,1)S(1)}, bf16[5,32,1024]{2,1,0:T(8,128)(2,1)S(1)}, u32[]{:S(2)}, u32[]{:S(2)}) collective-permute-start(bf16[5,32,1024]{2,1,0:T(8,128)(2,1)S(1)} %get-tuple-element.44), channel_id=1, source_target_pairs={{0,4},{4,8},{8,12},{1,5},{5,9},{9,13},{2,6},{6,10},{10,14},{3,7},{... | collective-permute-start | bytes 983048 | tf_op jit(solution)/shard_map/ppermute | solution.py:579
  9.6 10.2 %collective-permute-start.1 = (bf16[5,32,1024]{2,1,0:T(8,128)(2,1)S(1)}, bf16[5,32,1024]{2,1,0:T(8,128)(2,1)S(1)}, u32[]{:S(2)}, u32[]{:S(2)}) collective-permute-start(bf16[5,32,1024]{2,1,0:T(8,128)(2,1)S(1)} %get-tuple-element.45), channel_id=1, source_target_pairs={{4,0},{8,4},{12,8},{5,1},{9,5},{13,9},{6,2},{10,6},{14,10},{7,3},{... | collective-permute-start | bytes 983048 | tf_op jit(solution)/shard_map/ppermute | solution.py:580
  21.0 42.4 %collective-permute-start.2 = (bf16[58,32,128]{2,1,0:T(8,128)(2,1)}, bf16[58,32,128]{2,1,0:T(8,128)(2,1)}, u32[]{:S(2)}, u32[]{:S(2)}) collective-permute-start(bf16[58,32,128]{2,1,0:T(8,128)(2,1)} %get-tuple-element.47), channel_id=1, source_target_pairs={{0,1},{1,2},{2,3},{4,5},{5,6},{6,7},{8,9},{9,10},{10,11},{12,13},{... | collective-permute-start | bytes 1425416 | tf_op jit(solution)/shard_map/ppermute | solution.py:584
  24.8 38.6 %collective-permute-start.3 = (bf16[58,32,128]{2,1,0:T(8,128)(2,1)}, bf16[58,32,128]{2,1,0:T(8,128)(2,1)}, u32[]{:S(2)}, u32[]{:S(2)}) collective-permute-start(bf16[58,32,128]{2,1,0:T(8,128)(2,1)} %get-tuple-element.48), channel_id=1, source_target_pairs={{1,0},{2,1},{3,2},{5,4},{6,5},{7,6},{9,8},{10,9},{11,10},{13,12},{... | collective-permute-start | bytes 1425416 | tf_op jit(solution)/shard_map/ppermute | solution.py:585
  26.1 29.8 %all-to-all-start = ((f32[256,1,128]{2,1,0:T(1,128)}), f32[256,1,128]{2,1,0:T(1,128)S(1)}, u32[]{:S(2)}, u32[]{:S(2)}) async-start(f32[256,1,128]{2,1,0:T(1,128)} %get-tuple-element.37), calls=%async_computation | async-start | bytes 262144 | tf_op jit(solution)/shard_map/all_to_all | solution.py:537
  57.9 18.7 %all-to-all-start.1 = ((f32[256,1,128]{2,1,0:T(1,128)}), f32[256,1,128]{2,1,0:T(1,128)S(1)}, u32[]{:S(2)}, u32[]{:S(2)}) async-start(f32[256,1,128]{2,1,0:T(1,128)} %get-tuple-element.40), calls=%async_computation.1 | async-start | bytes 262144 | tf_op jit(solution)/shard_map/all_to_all | solution.py:537
  69.9 0.6 copy-start
  113.2 14.2 %all-to-all-start.4 = ((bf16[32,24,128]{2,1,0:T(8,128)(2,1)}), bf16[32,24,128]{2,1,0:T(8,128)(2,1)S(1)}, u32[]{:S(2)}, u32[]{:S(2)}) async-start(bf16[32,24,128]{2,1,0:T(8,128)(2,1)} %get-tuple-element.60), calls=%async_computation.4 | async-start | bytes 393216 | tf_op jit(solution)/shard_map/all_to_all | solution.py:537

commit v2 on v1

--- a/solution.py
+++ b/solution.py
@@ -102,8 +102,10 @@
 
 
 def arrived(ref):
-    total = jnp.sum(ref[...].reshape(ref.shape[0], 128), axis=0, keepdims=True)
-    return total
+    parts = [jnp.sum(ref[16 * n : 16 * n + 16], axis=0) for n in range(16)]
+    while len(parts) > 1:
+        parts = [a + b for a, b in zip(parts[::2], parts[1::2])]
+    return parts[0]
 
 
 def shifted(slab, lane):
@@ -118,7 +120,7 @@
 
 def spread_kernel(
     one_ref, two_ref, up_ref, vol_ref, c1_ref, c2_ref, ug_ref, vol3_out, down_ref, up_x_ref, stat_ref,
-    held, tmp, vol3, sems, out_sem,
+    held, vol3, sems, out_sem,
 ):
     sources = (("vol", vol_ref, None), ("c1", one_ref, c1_ref), ("c2", two_ref, c2_ref), ("ug", up_ref, ug_ref))
     copies = started([(src.at[0], held.at[n]) for n, (_, src, _) in enumerate(sources)], sems)
@@ -126,11 +128,11 @@
     parts = []
     for n, (name, _, dst) in enumerate(sources):
         copies[n].wait()
-        tmp[...] = held[n].reshape(C * B * B, Z).astype(F32)
         total, squares = jnp.zeros((C, Z), F32), jnp.zeros((C, Z), F32)
         for x in range(B):
+            turned_x = jnp.swapaxes(held[n, :, x].astype(F32), 0, 1)
             for y in range(B):
-                slab = tmp[pl.ds(x * B + y, C, stride=B * B), :]
+                slab = turned_x[y]
                 if name == "vol":
                     vol3[x, :, y * Z : (y + 1) * Z] = shifted(slab, lane).astype(BF16)
                     continue
@@ -167,7 +169,7 @@
 
 def extend_kernel(
     pos_ref, stat_ref, par_ref, c1_ref, c2_ref, slope_ref, xlow_ref, xhigh_ref, vol3_in, ylow_in, yhigh_in,
-    c1x_out, c2x_out, slopex_out, turn_out, act3_out, r_ref, c1x, c2x, slopex, turn, act3, ugx, vol3, sems, out_sems,
+    c1x_out, c2x_out, slopex_out, turn_out, act3_out, r_out, r_ref, c1x, c2x, slopex, turn, act3, ugx, vol3, sems, out_sems,
 ):
     target = {"c1": c1x, "c2": c2x, "ug": ugx}
     pairs = []
@@ -255,8 +257,9 @@
         lhs = jnp.concatenate([windows(c1x, x, 2, 2, B), inside], 0)
         return acc + lax.dot_general(lhs, vol3[x], TRANSPOSED, preferred_element_type=F32)
 
-    acc = lax.fori_loop(0, B, body, jnp.zeros((9 * C + 16, 3 * C), F32))
+    acc = lax.fori_loop(0, B, body, jnp.zeros((9 * C + 16, 3 * C), F32), unroll=2)
     r_ref[...] = turned(acc).astype(BF16)
+    leaving += started([(r_ref, r_out)], out_sems.at[pl.ds(5, 1)])
     for copy in leaving:
         copy.wait()
 
@@ -342,16 +345,35 @@
     return hi, mid, lo
 
 
+MARKS = 96
+
+
+def moved(row, lanes_up):
+    return pltpu.roll(row, lanes_up, axis=1) if lanes_up else row
+
+
+def sum_rows(sums):
+    lane = lax.broadcasted_iota(jnp.int32, (1, 128), 1)
+    hi, mid, lo = (jnp.where(lane < 64, part, 0.0) for part in three(sums))
+    return hi + moved(mid, 64), lo
+
+
+def sums_of(total):
+    return total[21:22] + moved(total[21:22], 64) + total[22:23]
+
+
 def middle_kernel(
-    pos_ref, got_ref, stat_ref, par_ref, w_in, c1x_in, c2x_in, slopex_in, turn_in, vol3_in, act3_in, r_in,
-    msg_ref, slope_ref, row_ref, w_ref, c1x_ref, c2x_ref, slopex_ref, turn_ref, vol3_ref, act3_ref, r_ref,
-    raw, grad, msg, sems,
+    pos_ref, got_ref, stat_ref, par_ref, raw, c1x_in, c2x_in, slopex_in, turn_in, vol3_in, act3_in, r_in,
+    msg_ref, slope_ref, row_ref, c1x_ref, w_ref, c2x_ref, slopex_ref, turn_ref, vol3_ref, act3_ref, r_ref,
+    grad, sems, row_sems,
 ):
+    cuts = [pl.ds(n * 3, 3) for n in range(4)]
+    early = started(
+        [(src.at[cut], dst.at[cut]) for cut in cuts for src, dst in ((slopex_in, slopex_ref), (c2x_in, c2x_ref))],
+        row_sems,
+    )
     arriving = started(
         [
-            (slopex_in, slopex_ref),
-            (c2x_in, c2x_ref),
-            (w_in, raw),
             (turn_in, turn_ref),
             (c1x_in, c1x_ref),
             (vol3_in, vol3_ref),
@@ -384,13 +406,13 @@
             grad[x, :, cut] = (value * keep).astype(BF16)
         return carry
 
+    as_matrix(raw, w_ref)
+    for n in range(4):
+        early[2 * n].wait()
+        early[2 * n + 1].wait()
+        lax.fori_loop(3 * n, 3 * n + 3, first, 0)
     arriving[0].wait()
     arriving[1].wait()
-    lax.fori_loop(0, B + 4, first, 0)
-    arriving[2].wait()
-    as_matrix(raw, w_ref)
-    arriving[3].wait()
-    arriving[4].wait()
     inside_y = {0: jnp.where(sy > 0, 1.0, 0.0), B + 1: jnp.where(sy < 3, 1.0, 0.0)}
 
     def second(x, acc):
@@ -411,7 +433,7 @@
         return b + bx * own_x, g + gsum * own_x
 
     zero = jnp.zeros((C, Z), F32)
-    b, g = lax.fori_loop(0, B + 2, second, (zero, zero))
+    b, g = lax.fori_loop(0, B + 2, second, (zero, zero), unroll=5)
 
     def third(x, acc):
         s, f = acc
@@ -419,34 +441,38 @@
         f = f + lax.dot_general(windows(grad, x, 3, 3, B), act3_ref[x], TRANSPOSED, preferred_element_type=F32)
         return s, f
 
-    for copy in arriving[5:]:
+    for copy in arriving[2:]:
         copy.wait()
     empty = jnp.zeros((9 * C, 3 * C), F32)
-    s, f = lax.fori_loop(0, B, third, (empty, empty))
+    s, f = lax.fori_loop(0, B, third, (empty, empty), unroll=4)
     sums = across(jnp.concatenate([b, g, zero, zero], 0))
-    hi, mid, lo = three(sums)
-    for m, part in enumerate((turned(s), r_ref[...].astype(F32), turned(f))):
+    rows = []
+    for marked, part in ((False, turned(s)), (True, r_ref[...].astype(F32)), (False, turned(f))):
+        packed = zero
         for kz in range(3):
-            for t in range(3):
-                msg[:, m * 9 + kz * 3 + t, :] = part[kz * C : (kz + 1) * C, t * 128 : (t + 1) * 128]
-    for i, part in enumerate((hi, mid, lo)):
-        msg[:, 27 + i, :] = jnp.broadcast_to(part, (C, 128))
-    msg[:, 30, :] = zero
-    msg[:, 31, :] = zero
-    msg_ref[...] = msg[...].astype(BF16)
+            band = part[kz * C : (kz + 1) * C]
+            rows += [band[:, 0:128][None], band[:, 128:256][None]]
+            end = band[:, 256:384]
+            packed += moved(jnp.where(lane < C, end, 0.0), kz * C)
+            if marked:
+                packed += moved(jnp.where((lane >= C) & (lane < C + 9), end, 0.0), MARKS - C + 9 * kz)
+        rows.append(packed[None])
+    rows += [jnp.broadcast_to(part, (C, 128))[None] for part in sum_rows(sums)] + [zero[None]]
+    for n in range(3):
+        block = jnp.swapaxes(jnp.concatenate(rows[8 * n : 8 * n + 8], 0), 0, 1)
+        msg_ref[:, 8 * n : 8 * n + 8, :] = block.astype(BF16)
 
 
 def relay_kernel(got_ref, out_ref):
     total = jnp.sum(got_ref[...].astype(F32), axis=0)
-    sums = total[27:28] + total[28:29] + total[29:30]
-    hi, mid, lo = three(sums)
-    out = jnp.concatenate([total[0:27], hi, mid, lo, total[30:32]], 0).astype(BF16)
+    first, second = sum_rows(sums_of(total))
+    out = jnp.concatenate([total[0:21], first, second, total[23:24]], 0).astype(BF16)
     out_ref[...] = jnp.broadcast_to(out[None], out_ref.shape)
 
 
 def share_kernel(got_ref, stat_ref, lanepar_ref, out_ref, row_ref):
     total = jnp.sum(got_ref[...].astype(F32), axis=0)
-    sums = total[27:28] + total[28:29] + total[29:30]
+    sums = sums_of(total)
     row_ref[...] = jnp.broadcast_to(sums, (8, 128))
     lane = lax.broadcasted_iota(jnp.int32, (1, 128), 1)
     stat = stat_ref[0:1]
@@ -459,32 +485,31 @@
     delta = alpha * sums * (1.0 / CELLS) - gamma * mean
     rows = jnp.where(lane < C, jnp.concatenate([alpha, gamma, delta], 0), 0.0)
     rows = jnp.concatenate([rows, jnp.zeros((5, 128), F32)], 0)
-    a = lax.broadcasted_iota(jnp.int32, (128, 384), 0)
-    o = lax.broadcasted_iota(jnp.int32, (128, 384), 1)
-    tile = jnp.where(o % C == a, 1.0, 0.0)
+    a = lax.broadcasted_iota(jnp.int32, (128, 896), 0)
+    o = lax.broadcasted_iota(jnp.int32, (128, 896), 1)
+    tile = jnp.where(o[:, 0:128] % C == a[:, 0:128], 1.0, 0.0)
     wide = jnp.dot(rows, tile, precision=lax.Precision.HIGHEST, preferred_element_type=F32)
-    spread = jnp.where((o // C + C == a) & (o < 9 * C), 1.0, 0.0)
-    marks = jnp.concatenate([total[11:12], total[14:15], total[17:18], jnp.zeros((5, 128), F32)], 0)
+    row = o // 128
+    block = (o % 128) // C
+    mark = jnp.where(row < 6, MARKS + 9 * (row // 2) + 4 * (row % 2) + block, MARKS + 9 * block + 8)
+    spread = jnp.where((mark == a) & ((row < 6) | (block < 3)), 1.0, 0.0)
+    marks = jnp.concatenate([total[13:14], jnp.zeros((7, 128), F32)], 0)
     ones = jnp.dot(marks, spread, precision=lax.Precision.HIGHEST, preferred_element_type=F32)
     parts = []
-    for kz in range(3):
-        for t in range(3):
-            cut = slice(t * 128, (t + 1) * 128)
-            one = (
-                wide[0:1, cut] * total[kz * 3 + t : kz * 3 + t + 1]
-                - wide[1:2, cut] * total[9 + kz * 3 + t : 10 + kz * 3 + t]
-                - wide[2:3, cut] * ones[kz : kz + 1, cut]
-            )
-            parts.append(one)
-    out = jnp.concatenate(parts + [total[18:27], jnp.zeros((6, 128), F32)], 0) * SCALE
+    for r in range(7):
+        parts.append(
+            wide[0:1] * total[r : r + 1]
+            - wide[1:2] * total[7 + r : 8 + r]
+            - wide[2:3] * ones[0:1, r * 128 : (r + 1) * 128]
+        )
+    out = jnp.concatenate(parts + [total[14:21], jnp.zeros((2, 128), F32)], 0) * SCALE
     out_ref[...] = jnp.broadcast_to(out.astype(BF16)[None], out_ref.shape)
 
 
 def last_kernel(
-    mask_ref, sum_ref, two_ref, stat_ref, par_ref, slope_ref, w_in, c1x_in,
-    out_ref, gain1_ref, bias1_ref, gain2_ref, bias2_ref, grad, tmp, w_ref, raw, c1x_ref, sems,
+    mask_ref, sum_ref, two_ref, stat_ref, par_ref, slope_ref, c1x_ref, raw,
+    out_ref, gain1_ref, bias1_ref, gain2_ref, bias2_ref, grad, done, w_ref, out_sems,
 ):
-    arriving = started([(w_in, raw), (c1x_in, c1x_ref)], sems)
     for ref, bias_ref, gain_ref in ((sum_ref, bias1_ref, gain1_ref), (two_ref, bias2_ref, gain2_ref)):
         scaled = ref[0:1] * SCALE
         bias_ref[...] = scaled[:, 0:C]
@@ -509,28 +534,30 @@
             grad[x, :, cut] = (value * keep).astype(BF16)
         return carry
 
-    for copy in arriving:
-        copy.wait()
     as_matrix(raw, w_ref)
     lax.fori_loop(0, B + 2, first, 0)
 
+    leaving = []
     for x in range(B):
         t = jnp.dot(w_ref[...], windows(grad, x, 2, 2, B), preferred_element_type=F32)
-        for y in range(B):
-            tmp[pl.ds(x * B + y, C, stride=B * B), :] = unshift(t, y, lane)
-    out_ref[0] = tmp[...].astype(BF16).reshape(C, B, B, Z)
-
-
-def filters_kernel(got_ref, one_ref, two_ref, tmp):
-    tmp[...] = got_ref[...].astype(F32)
+        rows = jnp.concatenate([unshift(t, y, lane)[None] for y in range(B)], 0)
+        done[x] = jnp.swapaxes(rows, 0, 1).astype(BF16)
+        leaving.append(pltpu.make_async_copy(done.at[x], out_ref.at[0, :, x], out_sems.at[x]))
+        leaving[-1].start()
+    for copy in leaving:
+        copy.wait()
+
+
+def filters_kernel(got_ref, one_ref, two_ref):
+    rows = jnp.swapaxes(got_ref[...].astype(F32), 0, 1)
     for m, ref in enumerate((one_ref, two_ref)):
         for kz in range(3):
-            for t in range(3):
-                slab = tmp[:, m * 9 + kz * 3 + t, :]
-                for i in range(4):
-                    k = 4 * t + i
-                    if k < 9:
-                        ref[k // 3, k % 3, kz] = slab[:, i * C : (i + 1) * C]
+            for k in range(9):
+                if k < 8:
+                    slab, i = rows[m * 7 + kz * 2 + k // 4], k % 4
+                else:
+                    slab, i = rows[m * 7 + 6], kz
+                ref[k // 3, k % 3, kz] = slab[:, i * C : (i + 1) * C]
 
 
 def exchanged(array, axes):
@@ -549,7 +576,6 @@
     three_fold = shaped((B, 3 * C, B * Z), BF16)
     near = shaped((B + 2, C, (B + 2) * Z), BF16)
     far = shaped((B + 4, C, (B + 4) * Z), BF16)
-    weights = shaped((3, 3, 3, C, C), BF16)
     near_wide, far_wide, block_wide = (shaped(a.shape, F32) for a in (near, far, block))
     row = shaped((8, 128), F32)
 
@@ -565,7 +591,6 @@
         [block, block, block, three_fold, along_x, along_x, everyone],
         scratch=[
             pltpu.VMEM((4, C, B, B, Z), BF16),
-            pltpu.VMEM((C * B * B, Z), F32),
             room(three_fold),
             sems(4),
             sems(1),
@@ -593,31 +618,31 @@
         extend_kernel,
         [near, far, far_wide, near_wide, three_fold, r_shape],
         scratch=[
-            room(near), room(far), room(far_wide), room(near_wide), room(three_fold), room(far), room(three_fold), sems(11), sems(5)
+            room(r_shape), room(near), room(far), room(far_wide), room(near_wide), room(three_fold), room(far), room(three_fold), sems(11), sems(6)
         ],
         flops=5 * 10**9,
         spaces=[SMEM] + [VMEM] * 7 + [HBM] * 3,
-        homes=[HBM] * 5 + [VMEM],
+        homes=[HBM] * 6,
         limit=16,
     )(pos, stat_row, par, c1, c2, slope_two, x_low, x_high, vol3, y_low, y_high)
 
-    terms, slope, row_two = call(
+    terms, slope, row_two, c1x_own = call(
         middle_kernel,
-        [shaped((32, 32, 128), BF16), near, row],
+        [shaped((32, 24, 128), BF16), near, row, near],
         scratch=[
-            pltpu.VMEM((3 * C, 9 * C), BF16), room(near), room(far), room(far_wide), room(near_wide), room(three_fold),
-            room(three_fold), room(r_shape), room(weights), room(far), pltpu.VMEM((32, 32, 128), F32), sems(8),
+            pltpu.VMEM((3 * C, 9 * C), BF16), room(far), room(far_wide), room(near_wide), room(three_fold),
+            room(three_fold), room(r_shape), room(far), sems(5), sems(8),
         ],
         flops=4 * 10**9,
-        spaces=[SMEM] + [VMEM] * 3 + [HBM] * 8,
+        spaces=[SMEM] + [VMEM] * 4 + [HBM] * 7,
         limit=18,
     )(pos, got_two, stat_row, par, weight_two, c1x, c2x, slopex, turn, vol3, act3, r)
 
     got_terms = exchanged(terms, PLANE)
-    relay = call(relay_kernel, shaped((8, 32, 128), BF16), spaces=[VMEM])(got_terms)
+    relay = call(relay_kernel, shaped((8, 24, 128), BF16), spaces=[VMEM])(got_terms)
     got_relay = exchanged(relay, "dp_0")
     shares, row_one = call(
-        share_kernel, [shaped((32, 24, 128), BF16), row], spaces=[VMEM] * 3
+        share_kernel, [shaped((32, 16, 128), BF16), row], spaces=[VMEM] * 3
     )(got_relay, stat_row, lanepar)
     got_shares = exchanged(shares, PLANE)
     vector = shaped((1, C), F32)
@@ -625,15 +650,16 @@
         last_kernel,
         [shaped((1, C, B, B, Z), BF16), vector, vector, vector, vector],
         scratch=[
-            room(near), pltpu.VMEM((C * B * B, Z), F32), pltpu.VMEM((3 * C, 9 * C), BF16), room(weights), room(near), sems(2)
+            room(near), pltpu.VMEM((B, C, B, Z), BF16), pltpu.VMEM((3 * C, 9 * C), BF16), sems(8)
         ],
         flops=4 * 10**9,
-        spaces=[SMEM] + [VMEM] * 5 + [HBM] * 2,
+        spaces=[SMEM] + [VMEM] * 7,
+        homes=[HBM] + [VMEM] * 4,
         limit=10,
-    )(pos, row_one, row_two, stat_row, par, slope, weight_one, c1x)
+    )(pos, row_one, row_two, stat_row, par, slope, c1x_own, weight_one)
     filters = shaped((3, 3, 3, C, C), F32)
     filter_one, filter_two = call(
-        filters_kernel, [filters, filters], scratch=[pltpu.VMEM((32, 24, 128), F32)], spaces=[VMEM]
+        filters_kernel, [filters, filters], spaces=[VMEM]
     )(got_shares)
     return (
         input_grad, filter_one, filter_two, gain_one_grad[0], bias_one_grad[0], gain_two_grad[0], bias_two_grad[0]

time: 129 us -> 124 us (0.961)
  Pallas kernels: 33 us -> 28.4 us
  waiting for transfers between devices: 30.6 us -> 32.2 us
    pallas_call x9, Pallas kernels: 33 us -> 28.4 us  [placed(): f(*[pltpu.with_memory_space_constraint(x, HBM) if space == HBM else x for...]
    all_to_all x3, waiting for transfers between devices: 21.7 us -> 23.2 us  [exchanged(): return lax.all_to_all(array, axes, 0, 0, tiled=True)]
where the time goes in v2:
time: 124 us; the launch traced here: 123 us
  starting transfers between devices  38.5 us (31%)
  waiting for transfers between devices  32.2 us (26%)
  Pallas kernels  28.4 us (23%)
  blocking collectives  23.1 us (19%)
    pallas_call x9, Pallas kernels, placed(): f(*[pltpu.with_memory_space_constraint(x, HBM) if space == HBM else x for...  28.4 us
    all_to_all x3, starting transfers between devices, exchanged(): return lax.all_to_all(array, axes, 0, 0, tiled=True)  27.9 us
    all_to_all x3, waiting for transfers between devices, exchanged(): return lax.all_to_all(array, axes, 0, 0, tiled=True)  23.2 us
    all_to_all x2, blocking collectives, exchanged(): return lax.all_to_all(array, axes, 0, 0, tiled=True)  23.1 us
    ppermute x1, waiting for transfers between devices, per_device(): x_low = lax.ppermute(send_up, 'sx', up)  5.06 us
    ppermute x1, starting transfers between devices, per_device(): x_low = lax.ppermute(send_up, 'sx', up)  4.17 us
    ppermute x1, starting transfers between devices, per_device(): y_low = lax.ppermute(send_up, 'sy', up)  3.88 us
    ppermute x1, waiting for transfers between devices, per_device(): x_high = lax.ppermute(send_down, 'sx', down_)  3.85 us
  transfers between devices with their start and end apart: 7, of which 5 were waited for; matrix products, arithmetic and copies ran while one was open for 0% of the time, Pallas kernels for 10%

profile of v2, /device:TPU:1, one launch (start us, length us, event | category | flops | bytes accessed | tf_op | source)
XLA Modules:
  0.0 123.3 jit_solution(7757855378699030513)
XLA Ops:
  0.6 3.4 %shard_map.153 = (bf16[8,32,1024]{2,1,0:T(8,128)(2,1)S(1)}, bf16[8,32,1024]{2,1,0:T(8,128)(2,1)S(1)}, bf16[8,32,1024]{2,1,0:T(8,128)(2,1)S(1)}, bf16[8,96,1024]{...) custom-call(bf16[1,32,8,8,128]{4,3,2,1,0:T(8,128)(2,1)} %one_ref.1, ...), custom_call_target="tpu_custom_call" | custom-call | bytes 1048576 | tf_op jit(solution)/shard_map/pallas_call | solution.py:75
  4.1 0.0 copy-start.2
  4.1 0.0 copy-start.3
  4.1 0.0 copy-start.4
  4.1 0.0 copy-start.5
  4.1 4.2 %collective-permute-start = (bf16[5,32,1024]{2,1,0:T(8,128)(2,1)S(1)}, bf16[5,32,1024]{2,1,0:T(8,128)(2,1)S(1)}, u32[]{:S(2)}, u32[]{:S(2)}) collective-permute-start(bf16[5,32,1024]{2,1,0:T(8,128)(2,1)S(1)} %get-tuple-element.45), channel_id=1, source_target_pairs={{0,4},{4,8},{8,12},{1,5},{5,9},{9,13},{2,6},{6,10},{10,14},{3,7},{... | collective-permute-start | bytes 983048 | tf_op jit(solution)/shard_map/ppermute | solution.py:604
  8.3 1.3 %collective-permute-start.1 = (bf16[5,32,1024]{2,1,0:T(8,128)(2,1)S(1)}, bf16[5,32,1024]{2,1,0:T(8,128)(2,1)S(1)}, u32[]{:S(2)}, u32[]{:S(2)}) collective-permute-start(bf16[5,32,1024]{2,1,0:T(8,128)(2,1)S(1)} %get-tuple-element.46), channel_id=1, source_target_pairs={{4,0},{8,4},{12,8},{5,1},{9,5},{13,9},{6,2},{10,6},{14,10},{7,3},{... | collective-permute-start | bytes 983048 | tf_op jit(solution)/shard_map/ppermute | solution.py:605
  9.6 5.1 %collective-permute-done.low_ref.xlow_ref = bf16[5,32,1024]{2,1,0:T(8,128)(2,1)S(1)} collective-permute-done((bf16[5,32,1024]{2,1,0:T(8,128)(2,1)S(1)}, bf16[5,32,1024]{2,1,0:T(8,128)(2,1)S(1)}, u32[]{:S(2)}, u32[]{:S(2)}) %collective-permute-start) | collective-permute-done | bytes 327712 | tf_op jit(solution)/shard_map/ppermute | solution.py:604
  14.7 3.9 %collective-permute-done.1.high_ref.xhigh_ref = bf16[5,32,1024]{2,1,0:T(8,128)(2,1)S(1)} collective-permute-done((bf16[5,32,1024]{2,1,0:T(8,128)(2,1)S(1)}, bf16[5,32,1024]{2,1,0:T(8,128)(2,1)S(1)}, u32[]{:S(2)}, u32[]{:S(2)}) %collective-permute-start.1) | collective-permute-done | bytes 327712 | tf_op jit(solution)/shard_map/ppermute | solution.py:605
  18.5 1.1 shard_map.155
  19.6 3.9 %collective-permute-start.2 = (bf16[58,32,128]{2,1,0:T(8,128)(2,1)}, bf16[58,32,128]{2,1,0:T(8,128)(2,1)}, u32[]{:S(2)}, u32[]{:S(2)}) collective-permute-start(bf16[58,32,128]{2,1,0:T(8,128)(2,1)} %get-tuple-element.48), channel_id=1, source_target_pairs={{0,1},{1,2},{2,3},{4,5},{5,6},{6,7},{8,9},{9,10},{10,11},{12,13},{... | collective-permute-start | bytes 1425416 | tf_op jit(solution)/shard_map/ppermute | solution.py:609
  23.5 1.3 %collective-permute-start.3 = (bf16[58,32,128]{2,1,0:T(8,128)(2,1)}, bf16[58,32,128]{2,1,0:T(8,128)(2,1)}, u32[]{:S(2)}, u32[]{:S(2)}) collective-permute-start(bf16[58,32,128]{2,1,0:T(8,128)(2,1)} %get-tuple-element.49), channel_id=1, source_target_pairs={{1,0},{2,1},{3,2},{5,4},{6,5},{7,6},{9,8},{10,9},{11,10},{13,12},{... | collective-permute-start | bytes 1425416 | tf_op jit(solution)/shard_map/ppermute | solution.py:610
  24.8 16.8 %all-to-all-start = ((f32[256,1,128]{2,1,0:T(1,128)}), f32[256,1,128]{2,1,0:T(1,128)S(1)}, u32[]{:S(2)}, u32[]{:S(2)}) async-start(f32[256,1,128]{2,1,0:T(1,128)} %get-tuple-element.38), calls=%async_computation | async-start | bytes 262144 | tf_op jit(solution)/shard_map/all_to_all | solution.py:564
  41.6 0.1 pad_add_fusion.pos_ref.mask_ref
  41.7 0.1 pad_maximum_fusion
  41.8 12.8 %all-to-all-done.got_ref = f32[256,1,128]{2,1,0:T(1,128)S(1)} async-done(((f32[256,1,128]{2,1,0:T(1,128)}), f32[256,1,128]{2,1,0:T(1,128)S(1)}, u32[]{:S(2)}, u32[]{:S(2)}) %all-to-all-start) | async-done | bytes 131104 | tf_op jit(solution)/shard_map/all_to_all | solution.py:564
  54.6 0.1 broadcast_in_dim.4.par_ref
  54.7 1.8 %shard_map.154 = (f32[256,1,128]{2,1,0:T(1,128)}, f32[8,128]{1,0:T(8,128)S(1)}, f32[8,32,1024]{2,1,0:T(8,128)S(1)}) custom-call(f32[256,1,128]{2,1,0:T(1,128)S(1)} %all-to-all-done.got_ref, f32[128,128]{1,0:T(8,128)S(1)} %broadcast_in_dim.4.par_ref, bf16[8,32,1024]{2,1,0:T(8,128)(2,1)S(1)} %get-tuple-element.39.c2_ref, ...), custom_call_target="tpu_custom_call" | custom-call | bytes 1048576 | tf_op jit(solution)/shard_map/pallas_call | solution.py:75
  56.5 5.5 %all-to-all-start.1 = ((f32[256,1,128]{2,1,0:T(1,128)}), f32[256,1,128]{2,1,0:T(1,128)S(1)}, u32[]{:S(2)}, u32[]{:S(2)}) async-start(f32[256,1,128]{2,1,0:T(1,128)} %get-tuple-element.41), calls=%async_computation.1 | async-start | bytes 262144 | tf_op jit(solution)/shard_map/all_to_all | solution.py:564
  62.0 0.0 collective-permute-done.3.yhigh_in
  62.0 0.0 copy-start
  62.0 6.4 %shard_map.156 = (bf16[10,32,1280]{2,1,0:T(8,128)(2,1)}, bf16[12,32,1536]{2,1,0:T(8,128)(2,1)}, f32[12,32,1536]{2,1,0:T(8,128)}, f32[10,32,1280]{2,1,0:T(8,128)}...) custom-call(s32[2]{0:T(128)S(1)} %pad_add_fusion.pos_ref.mask_ref, f32[8,128]{1,0:T(8,128)S(1)} %get-tuple-element.42.stat_ref, ...), custom_call_target="tpu_custom_call" | custom-call | flops 5000000000 | bytes 1048576 | tf_op jit(solution)/shard_map/pallas_call | solution.py:75
  68.4 6.7 %all-to-all-done.1.got_ref = f32[256,1,128]{2,1,0:T(1,128)S(1)} async-done(((f32[256,1,128]{2,1,0:T(1,128)}), f32[256,1,128]{2,1,0:T(1,128)S(1)}, u32[]{:S(2)}, u32[]{:S(2)}) %all-to-all-start.1) | async-done | bytes 131104 | tf_op jit(solution)/shard_map/all_to_all | solution.py:564
  75.1 9.5 %shard_map.157 = (bf16[32,24,128]{2,1,0:T(8,128)(2,1)S(1)}, bf16[10,32,1280]{2,1,0:T(8,128)(2,1)S(1)}, f32[8,128]{1,0:T(8,128)S(1)}, bf16[10,32,1280]{2,1,0:T(8,128)(2,1)S(1)}) custom-call(s32[2]{0:T(128)S(1)} %pad_add_fusion.pos_ref.mask_ref, f32[256,1,128]{2,1,0:T(1,128)S(1)} %all-to-all-done.1.got_ref, f32[8,128]{1,0:T(8,128)S(1)} %get-tuple-element.42.stat_ref, ...), custom_call_target="tpu_custom_call" | custom-call | flops 4000000000 | bytes 1048576 | tf_op jit(solution)/shard_map/pallas_call | solution.py:75
  84.6 11.5 %all_to_all.25.got_ref = bf16[32,24,128]{2,1,0:T(8,128)(2,1)S(1)} all-to-all(bf16[32,24,128]{2,1,0:T(8,128)(2,1)S(1)} %get-tuple-element.56), channel_id=1, replica_groups=mesh['dp_0'=8,'dp_1'=2,'sx'=4,'sy'=4] {'dp_1','sx','sy'}, dimensions={0} | all-to-all | bytes 393216 | tf_op jit(solution)/shard_map/all_to_all | solution.py:564
  96.2 0.2 shard_map.158
  96.4 11.6 %all_to_all.26.got_ref = bf16[8,24,128]{2,1,0:T(8,128)(2,1)S(1)} all-to-all(bf16[8,24,128]{2,1,0:T(8,128)(2,1)S(1)} %shard_map.158), channel_id=1, replica_groups=mesh['dp_0'=8,'dp_1'=2,'sx'=4,'sy'=4] {'dp_0'}, dimensions={0} | all-to-all | bytes 98304 | tf_op jit(solution)/shard_map/all_to_all | solution.py:564
  108.0 1.2 shard_map.159
  109.2 5.5 %all-to-all-start.4 = ((bf16[32,16,128]{2,1,0:T(8,128)(2,1)}), bf16[32,16,128]{2,1,0:T(8,128)(2,1)S(1)}, u32[]{:S(2)}, u32[]{:S(2)}) async-start(bf16[32,16,128]{2,1,0:T(8,128)(2,1)} %get-tuple-element.62), calls=%async_computation.4 | async-start | bytes 262144 | tf_op jit(solution)/shard_map/all_to_all | solution.py:564
  114.7 3.8 %shard_map.160 = (bf16[1,32,8,8,128]{4,3,2,1,0:T(8,128)(2,1)}, f32[1,32]{1,0:T(1,128)}, f32[1,32]{1,0:T(1,128)}, f32[1,32]{1,0:T(1,128)}, f32[1,32]{1,0:T(1,128)}) custom-call(s32[2]{0:T(128)S(1)} %pad_add_fusion.pos_ref.mask_ref, f32[8,128]{1,0:T(8,128)S(1)} %get-tuple-element.57.sum_ref, f32[8,128]{1,0:T(8,128)S(1)} %get-tuple-element.58.two_ref, ...), custom_call_target="tpu_custom_call" | custom-call | flops 4000000000 | bytes 1048576 | tf_op jit(solution)/shard_map/pallas_call | solution.py:75
  118.5 3.7 %all-to-all-done.4.got_ref = bf16[32,16,128]{2,1,0:T(8,128)(2,1)S(1)} async-done(((bf16[32,16,128]{2,1,0:T(8,128)(2,1)}), bf16[32,16,128]{2,1,0:T(8,128)(2,1)S(1)}, u32[]{:S(2)}, u32[]{:S(2)}) %all-to-all-start.4) | async-done | bytes 131104 | tf_op jit(solution)/shard_map/all_to_all | solution.py:564
  122.2 1.1 shard_map.161
  (9 shorter events, 0.0 us)
Async XLA Ops:
  4.1 37.6 %copy-start.2 = (f32[32]{0:T(128)S(1)}, f32[32]{0:T(128)}, u32[]{:S(2)}) copy-start(f32[32]{0:T(128)} %param.19) | copy-start | bytes 388
  4.1 37.6 %copy-start.3 = (f32[32]{0:T(128)S(1)}, f32[32]{0:T(128)}, u32[]{:S(2)}) copy-start(f32[32]{0:T(128)} %param.18) | copy-start | bytes 388
  4.1 37.6 %copy-start.4 = (f32[32]{0:T(128)S(1)}, f32[32]{0:T(128)}, u32[]{:S(2)}) copy-start(f32[32]{0:T(128)} %param.17) | copy-start | bytes 388
  4.1 37.6 %copy-start.5 = (f32[32]{0:T(128)S(1)}, f32[32]{0:T(128)}, u32[]{:S(2)}) copy-start(f32[32]{0:T(128)} %param.16) | copy-start | bytes 388
  4.1 10.5 %collective-permute-start = (bf16[5,32,1024]{2,1,0:T(8,128)(2,1)S(1)}, bf16[5,32,1024]{2,1,0:T(8,128)(2,1)S(1)}, u32[]{:S(2)}, u32[]{:S(2)}) collective-permute-start(bf16[5,32,1024]{2,1,0:T(8,128)(2,1)S(1)} %get-tuple-element.45), channel_id=1, source_target_pairs={{0,4},{4,8},{8,12},{1,5},{5,9},{9,13},{2,6},{6,10},{10,14},{3,7},{... | collective-permute-start | bytes 983048 | tf_op jit(solution)/shard_map/ppermute | solution.py:604
  8.3 10.2 %collective-permute-start.1 = (bf16[5,32,1024]{2,1,0:T(8,128)(2,1)S(1)}, bf16[5,32,1024]{2,1,0:T(8,128)(2,1)S(1)}, u32[]{:S(2)}, u32[]{:S(2)}) collective-permute-start(bf16[5,32,1024]{2,1,0:T(8,128)(2,1)S(1)} %get-tuple-element.46), channel_id=1, source_target_pairs={{4,0},{8,4},{12,8},{5,1},{9,5},{13,9},{6,2},{10,6},{14,10},{7,3},{... | collective-permute-start | bytes 983048 | tf_op jit(solution)/shard_map/ppermute | solution.py:605
  19.6 42.4 %collective-permute-start.2 = (bf16[58,32,128]{2,1,0:T(8,128)(2,1)}, bf16[58,32,128]{2,1,0:T(8,128)(2,1)}, u32[]{:S(2)}, u32[]{:S(2)}) collective-permute-start(bf16[58,32,128]{2,1,0:T(8,128)(2,1)} %get-tuple-element.48), channel_id=1, source_target_pairs={{0,1},{1,2},{2,3},{4,5},{5,6},{6,7},{8,9},{9,10},{10,11},{12,13},{... | collective-permute-start | bytes 1425416 | tf_op jit(solution)/shard_map/ppermute | solution.py:609
  23.5 38.5 %collective-permute-start.3 = (bf16[58,32,128]{2,1,0:T(8,128)(2,1)}, bf16[58,32,128]{2,1,0:T(8,128)(2,1)}, u32[]{:S(2)}, u32[]{:S(2)}) collective-permute-start(bf16[58,32,128]{2,1,0:T(8,128)(2,1)} %get-tuple-element.49), channel_id=1, source_target_pairs={{1,0},{2,1},{3,2},{5,4},{6,5},{7,6},{9,8},{10,9},{11,10},{13,12},{... | collective-permute-start | bytes 1425416 | tf_op jit(solution)/shard_map/ppermute | solution.py:610
  24.8 29.8 %all-to-all-start = ((f32[256,1,128]{2,1,0:T(1,128)}), f32[256,1,128]{2,1,0:T(1,128)S(1)}, u32[]{:S(2)}, u32[]{:S(2)}) async-start(f32[256,1,128]{2,1,0:T(1,128)} %get-tuple-element.38), calls=%async_computation | async-start | bytes 262144 | tf_op jit(solution)/shard_map/all_to_all | solution.py:564
  56.5 18.7 %all-to-all-start.1 = ((f32[256,1,128]{2,1,0:T(1,128)}), f32[256,1,128]{2,1,0:T(1,128)S(1)}, u32[]{:S(2)}, u32[]{:S(2)}) async-start(f32[256,1,128]{2,1,0:T(1,128)} %get-tuple-element.41), calls=%async_computation.1 | async-start | bytes 262144 | tf_op jit(solution)/shard_map/all_to_all | solution.py:564
  62.0 13.1 %copy-start = (bf16[3,3,3,32,32]{4,3,2,1,0:T(8,128)(2,1)S(1)}, bf16[3,3,3,32,32]{4,3,2,1,0:T(8,128)(2,1)}, u32[]{:S(2)}) copy-start(bf16[3,3,3,32,32]{4,3,2,1,0:T(8,128)(2,1)} %raw.2) | copy-start | bytes 165892
  75.1 39.6 %copy-start.1 = (bf16[3,3,3,32,32]{4,3,2,1,0:T(8,128)(2,1)S(1)}, bf16[3,3,3,32,32]{4,3,2,1,0:T(8,128)(2,1)}, u32[]{:S(2)}) copy-start(bf16[3,3,3,32,32]{4,3,2,1,0:T(8,128)(2,1)} %raw.3) | copy-start | bytes 165892
  109.2 13.1 %all-to-all-start.4 = ((bf16[32,16,128]{2,1,0:T(8,128)(2,1)}), bf16[32,16,128]{2,1,0:T(8,128)(2,1)S(1)}, u32[]{:S(2)}, u32[]{:S(2)}) async-start(bf16[32,16,128]{2,1,0:T(8,128)(2,1)} %get-tuple-element.62), calls=%async_computation.4 | async-start | bytes 262144 | tf_op jit(solution)/shard_map/all_to_all | solution.py:564

commit v3 on v2

--- a/solution.py
+++ b/solution.py
@@ -168,7 +168,7 @@
 
 
 def extend_kernel(
-    pos_ref, stat_ref, par_ref, c1_ref, c2_ref, slope_ref, xlow_ref, xhigh_ref, vol3_in, ylow_in, yhigh_in,
+    pos_ref, stat_ref, par_ref, c1_ref, xlow_ref, xhigh_ref, vol3_in, ylow_in, yhigh_in,
     c1x_out, c2x_out, slopex_out, turn_out, act3_out, r_out, r_ref, c1x, c2x, slopex, turn, act3, ugx, vol3, sems, out_sems,
 ):
     target = {"c1": c1x, "c2": c2x, "ug": ugx}
@@ -194,17 +194,16 @@
 
     lax.fori_loop(0, B, activation, 0)
     leaving = started([(act3, act3_out)], out_sems)
-    for f, w, own in (("c1", 1, c1_ref), ("c2", 2, c2_ref)):
-        for x in range(B):
-            target[f][x + w, :, w * Z : (w + B) * Z] = own[x]
+    for x in range(B):
+        c1x[x + 1, :, Z : (1 + B) * Z] = c1_ref[x]
     width = dict(FIELDS)
     for side, ref in ((-1, xlow_ref), (1, xhigh_ref)):
         for i, (f, x) in enumerate(places_x(side)):
             w = width[f]
             target[f][x, :, w * Z : (w + B) * Z] = ref[i]
-    for copy in arriving:
+    for copy in arriving[:-1]:
         copy.wait()
-    leaving += started([(c1x, c1x_out), (c2x, c2x_out)], out_sems.at[pl.ds(1, 2)])
+    leaving += started([(c1x, c1x_out)] + [(c2x.at[cut], c2x_out.at[cut]) for cut in RIM], out_sems.at[pl.ds(1, 5)])
 
     def slope_at(x, y):
         cut = slice(y * Z, (y + 1) * Z)
@@ -222,11 +221,10 @@
     def between(x, carry):
         for y in (0, 1, B + 2, B + 3):
             slope_at(x + 2, y)
-        slopex[x + 2, :, 2 * Z : (2 + B) * Z] = slope_ref[x]
         return carry
 
     lax.fori_loop(0, B, between, 0)
-    leaving += started([(slopex, slopex_out)], out_sems.at[pl.ds(3, 1)])
+    leaving += started([(slopex.at[cut], slopex_out.at[cut]) for cut in RIM], out_sems.at[pl.ds(6, 4)])
 
     def turn_at(x, y):
         cut = slice(y * Z, (y + 1) * Z)
@@ -243,7 +241,7 @@
         return carry
 
     lax.fori_loop(0, B, sides, 0)
-    leaving += started([(turn, turn_out)], out_sems.at[pl.ds(4, 1)])
+    leaving += started([(turn, turn_out)], out_sems.at[pl.ds(10, 1)])
 
     sx, sy = pos_ref[0], pos_ref[1]
     row = lax.broadcasted_iota(jnp.int32, (16, B * Z), 0)
@@ -257,12 +255,20 @@
         lhs = jnp.concatenate([windows(c1x, x, 2, 2, B), inside], 0)
         return acc + lax.dot_general(lhs, vol3[x], TRANSPOSED, preferred_element_type=F32)
 
+    arriving[-1].wait()
     acc = lax.fori_loop(0, B, body, jnp.zeros((9 * C + 16, 3 * C), F32), unroll=2)
     r_ref[...] = turned(acc).astype(BF16)
-    leaving += started([(r_ref, r_out)], out_sems.at[pl.ds(5, 1)])
+    leaving += started([(r_ref, r_out)], out_sems.at[pl.ds(11, 1)])
     for copy in leaving:
         copy.wait()
 
+
+RIM = (
+    (pl.ds(0, 2),),
+    (pl.ds(B + 2, 2),),
+    (pl.ds(2, B), slice(None), pl.ds(0, 2 * Z)),
+    (pl.ds(2, B), slice(None), pl.ds((B + 2) * Z, 2 * Z)),
+)
 
 TRANSPOSED = (((1,), (1,)), ((), ()))
 
@@ -363,13 +369,12 @@
 
 
 def middle_kernel(
-    pos_ref, got_ref, stat_ref, par_ref, raw, c1x_in, c2x_in, slopex_in, turn_in, vol3_in, act3_in, r_in,
-    msg_ref, slope_ref, row_ref, c1x_ref, w_ref, c2x_ref, slopex_ref, turn_ref, vol3_ref, act3_ref, r_ref,
+    pos_ref, got_ref, stat_ref, par_ref, raw, c2_ref, slope_two_ref, c1x_in, c2x_in, slopex_in, turn_in, vol3_in, act3_in, r_in,
+    msg_ref, slope_ref, row_ref, w_ref, c1x_ref, c2x_ref, slopex_ref, turn_ref, vol3_ref, act3_ref, r_ref,
     grad, sems, row_sems,
 ):
-    cuts = [pl.ds(n * 3, 3) for n in range(4)]
     early = started(
-        [(src.at[cut], dst.at[cut]) for cut in cuts for src, dst in ((slopex_in, slopex_ref), (c2x_in, c2x_ref))],
+        [(src.at[cut], dst.at[cut]) for cut in RIM for src, dst in ((slopex_in, slopex_ref), (c2x_in, c2x_ref))],
         row_sems,
     )
     arriving = started(
@@ -396,21 +401,43 @@
         for y in (0, 1, B + 2, B + 3)
     }
 
-    def first(x, carry):
+    def own(x, carry):
+        for y in range(B):
+            cut = slice(y * Z, (y + 1) * Z)
+            value = amp * slope_two_ref[x, :, cut] - by * c2_ref[x, :, cut].astype(F32) - off
+            grad[x + 2, :, (y + 2) * Z : (y + 3) * Z] = value.astype(BF16)
+        return carry
+
+    lax.fori_loop(0, B, own, 0, unroll=2)
+    as_matrix(raw, w_ref)
+
+    def rim_at(x, y, inside_x):
+        cut = slice(y * Z, (y + 1) * Z)
+        value = amp * slopex_ref[x, :, cut] - by * c2x_ref[x, :, cut].astype(F32) - off
+        keep = inside_x * inside_y[y] if y in inside_y else inside_x
+        grad[x, :, cut] = (value * keep).astype(BF16)
+
+    for copy in early[:4]:
+        copy.wait()
+
+    def ends(i, carry):
+        x = jnp.where(i < 2, i, i + B)
         gx = sx * B + x - 2
         inside_x = jnp.where((gx >= 0) & (gx < 4 * B), 1.0, 0.0)
         for y in range(B + 4):
-            cut = slice(y * Z, (y + 1) * Z)
-            value = amp * slopex_ref[x, :, cut] - by * c2x_ref[x, :, cut].astype(F32) - off
-            keep = inside_x * inside_y[y] if y in inside_y else inside_x
-            grad[x, :, cut] = (value * keep).astype(BF16)
+            rim_at(x, y, inside_x)
         return carry
 
-    as_matrix(raw, w_ref)
-    for n in range(4):
-        early[2 * n].wait()
-        early[2 * n + 1].wait()
-        lax.fori_loop(3 * n, 3 * n + 3, first, 0)
+    lax.fori_loop(0, 4, ends, 0)
+    for copy in early[4:]:
+        copy.wait()
+
+    def sides(x, carry):
+        for y in (0, 1, B + 2, B + 3):
+            rim_at(x + 2, y, 1.0)
+        return carry
+
+    lax.fori_loop(0, B, sides, 0)
     arriving[0].wait()
     arriving[1].wait()
     inside_y = {0: jnp.where(sy > 0, 1.0, 0.0), B + 1: jnp.where(sy < 3, 1.0, 0.0)}
@@ -470,6 +497,12 @@
     out_ref[...] = jnp.broadcast_to(out[None], out_ref.shape)
 
 
+def selected(rows, choice):
+    parts = jnp.concatenate(three(rows), 0).astype(BF16)
+    out = jnp.dot(parts, choice.astype(BF16), preferred_element_type=F32)
+    return out[0:8] + out[8:16] + out[16:24]
+
+
 def share_kernel(got_ref, stat_ref, lanepar_ref, out_ref, row_ref):
     total = jnp.sum(got_ref[...].astype(F32), axis=0)
     sums = sums_of(total)
@@ -488,13 +521,13 @@
     a = lax.broadcasted_iota(jnp.int32, (128, 896), 0)
     o = lax.broadcasted_iota(jnp.int32, (128, 896), 1)
     tile = jnp.where(o[:, 0:128] % C == a[:, 0:128], 1.0, 0.0)
-    wide = jnp.dot(rows, tile, precision=lax.Precision.HIGHEST, preferred_element_type=F32)
+    wide = selected(rows, tile)
     row = o // 128
     block = (o % 128) // C
     mark = jnp.where(row < 6, MARKS + 9 * (row // 2) + 4 * (row % 2) + block, MARKS + 9 * block + 8)
     spread = jnp.where((mark == a) & ((row < 6) | (block < 3)), 1.0, 0.0)
     marks = jnp.concatenate([total[13:14], jnp.zeros((7, 128), F32)], 0)
-    ones = jnp.dot(marks, spread, precision=lax.Precision.HIGHEST, preferred_element_type=F32)
+    ones = selected(marks, spread)
     parts = []
     for r in range(7):
         parts.append(
@@ -507,9 +540,10 @@
 
 
 def last_kernel(
-    mask_ref, sum_ref, two_ref, stat_ref, par_ref, slope_ref, c1x_ref, raw,
-    out_ref, gain1_ref, bias1_ref, gain2_ref, bias2_ref, grad, done, w_ref, out_sems,
+    mask_ref, sum_ref, two_ref, stat_ref, par_ref, slope_ref, raw, c1x_in,
+    out_ref, gain1_ref, bias1_ref, gain2_ref, bias2_ref, grad, done, w_ref, c1x_ref, out_sems, sems,
 ):
+    arriving = started([(c1x_in, c1x_ref)], sems)
     for ref, bias_ref, gain_ref in ((sum_ref, bias1_ref, gain1_ref), (two_ref, bias2_ref, gain2_ref)):
         scaled = ref[0:1] * SCALE
         bias_ref[...] = scaled[:, 0:C]
@@ -535,6 +569,7 @@
         return carry
 
     as_matrix(raw, w_ref)
+    arriving[0].wait()
     lax.fori_loop(0, B + 2, first, 0)
 
     leaving = []
@@ -618,25 +653,25 @@
         extend_kernel,
         [near, far, far_wide, near_wide, three_fold, r_shape],
         scratch=[
-            room(r_shape), room(near), room(far), room(far_wide), room(near_wide), room(three_fold), room(far), room(three_fold), sems(11), sems(6)
+            room(r_shape), room(near), room(far), room(far_wide), room(near_wide), room(three_fold), room(far), room(three_fold), sems(11), sems(12)
         ],
         flops=5 * 10**9,
-        spaces=[SMEM] + [VMEM] * 7 + [HBM] * 3,
+        spaces=[SMEM] + [VMEM] * 5 + [HBM] * 3,
         homes=[HBM] * 6,
         limit=16,
-    )(pos, stat_row, par, c1, c2, slope_two, x_low, x_high, vol3, y_low, y_high)
-
-    terms, slope, row_two, c1x_own = call(
+    )(pos, stat_row, par, c1, x_low, x_high, vol3, y_low, y_high)
+
+    terms, slope, row_two = call(
         middle_kernel,
-        [shaped((32, 24, 128), BF16), near, row, near],
+        [shaped((32, 24, 128), BF16), near, row],
         scratch=[
-            pltpu.VMEM((3 * C, 9 * C), BF16), room(far), room(far_wide), room(near_wide), room(three_fold),
+            pltpu.VMEM((3 * C, 9 * C), BF16), room(near), room(far), room(far_wide), room(near_wide), room(three_fold),
             room(three_fold), room(r_shape), room(far), sems(5), sems(8),
         ],
         flops=4 * 10**9,
-        spaces=[SMEM] + [VMEM] * 4 + [HBM] * 7,
+        spaces=[SMEM] + [VMEM] * 6 + [HBM] * 7,
         limit=18,
-    )(pos, got_two, stat_row, par, weight_two, c1x, c2x, slopex, turn, vol3, act3, r)
+    )(pos, got_two, stat_row, par, weight_two, c2, slope_two, c1x, c2x, slopex, turn, vol3, act3, r)
 
     got_terms = exchanged(terms, PLANE)
     relay = call(relay_kernel, shaped((8, 24, 128), BF16), spaces=[VMEM])(got_terms)
@@ -650,13 +685,13 @@
         last_kernel,
         [shaped((1, C, B, B, Z), BF16), vector, vector, vector, vector],
         scratch=[
-            room(near), pltpu.VMEM((B, C, B, Z), BF16), pltpu.VMEM((3 * C, 9 * C), BF16), sems(8)
+            room(near), pltpu.VMEM((B, C, B, Z), BF16), pltpu.VMEM((3 * C, 9 * C), BF16), room(near), sems(8), sems(1)
         ],
         flops=4 * 10**9,
-        spaces=[SMEM] + [VMEM] * 7,
+        spaces=[SMEM] + [VMEM] * 6 + [HBM],
         homes=[HBM] + [VMEM] * 4,
         limit=10,
-    )(pos, row_one, row_two, stat_row, par, slope, c1x_own, weight_one)
+    )(pos, row_one, row_two, stat_row, par, slope, weight_one, c1x)
     filters = shaped((3, 3, 3, C, C), F32)
     filter_one, filter_two = call(
         filters_kernel, [filters, filters], spaces=[VMEM]

time: 124 us -> 123 us (level)
  no operation moved by 1% of the time
where the time goes in v3:
time: 123 us; the launch traced here: 122 us
  starting transfers between devices  38.5 us (31%)
  waiting for transfers between devices  31.6 us (26%)
  Pallas kernels  28.4 us (23%)
  blocking collectives  22.7 us (18%)
    pallas_call x9, Pallas kernels, placed(): f(*[pltpu.with_memory_space_constraint(x, HBM) if space == HBM else x for...  28.4 us
    all_to_all x3, starting transfers between devices, exchanged(): return lax.all_to_all(array, axes, 0, 0, tiled=True)  27.9 us
    all_to_all x2, blocking collectives, exchanged(): return lax.all_to_all(array, axes, 0, 0, tiled=True)  22.7 us
    all_to_all x3, waiting for transfers between devices, exchanged(): return lax.all_to_all(array, axes, 0, 0, tiled=True)  22.7 us
    ppermute x1, waiting for transfers between devices, per_device(): x_low = lax.ppermute(send_up, 'sx', up)  5.06 us
    ppermute x1, starting transfers between devices, per_device(): x_low = lax.ppermute(send_up, 'sx', up)  4.17 us
    ppermute x1, starting transfers between devices, per_device(): y_low = lax.ppermute(send_up, 'sy', up)  3.88 us
    ppermute x1, waiting for transfers between devices, per_device(): x_high = lax.ppermute(send_down, 'sx', down_)  3.85 us
  transfers between devices with their start and end apart: 7, of which 5 were waited for; matrix products, arithmetic and copies ran while one was open for 0% of the time, Pallas kernels for 10%

profile of v3, /device:TPU:1, one launch (start us, length us, event | category | flops | bytes accessed | tf_op | source)
XLA Modules:
  0.0 122.3 jit_solution(8351106335085589989)
XLA Ops:
  0.6 3.4 %shard_map.153 = (bf16[8,32,1024]{2,1,0:T(8,128)(2,1)S(1)}, bf16[8,32,1024]{2,1,0:T(8,128)(2,1)S(1)}, bf16[8,32,1024]{2,1,0:T(8,128)(2,1)S(1)}, bf16[8,96,1024]{...) custom-call(bf16[1,32,8,8,128]{4,3,2,1,0:T(8,128)(2,1)} %one_ref.1, ...), custom_call_target="tpu_custom_call" | custom-call | bytes 1048576 | tf_op jit(solution)/shard_map/pallas_call | solution.py:75
  4.1 0.0 copy-start.2
  4.1 0.0 copy-start.3
  4.1 0.0 copy-start.4
  4.1 0.0 copy-start.5
  4.1 4.2 %collective-permute-start = (bf16[5,32,1024]{2,1,0:T(8,128)(2,1)S(1)}, bf16[5,32,1024]{2,1,0:T(8,128)(2,1)S(1)}, u32[]{:S(2)}, u32[]{:S(2)}) collective-permute-start(bf16[5,32,1024]{2,1,0:T(8,128)(2,1)S(1)} %get-tuple-element.44), channel_id=1, source_target_pairs={{0,4},{4,8},{8,12},{1,5},{5,9},{9,13},{2,6},{6,10},{10,14},{3,7},{... | collective-permute-start | bytes 983048 | tf_op jit(solution)/shard_map/ppermute | solution.py:639
  8.3 1.3 %collective-permute-start.1 = (bf16[5,32,1024]{2,1,0:T(8,128)(2,1)S(1)}, bf16[5,32,1024]{2,1,0:T(8,128)(2,1)S(1)}, u32[]{:S(2)}, u32[]{:S(2)}) collective-permute-start(bf16[5,32,1024]{2,1,0:T(8,128)(2,1)S(1)} %get-tuple-element.45), channel_id=1, source_target_pairs={{4,0},{8,4},{12,8},{5,1},{9,5},{13,9},{6,2},{10,6},{14,10},{7,3},{... | collective-permute-start | bytes 983048 | tf_op jit(solution)/shard_map/ppermute | solution.py:640
  9.6 5.1 %collective-permute-done.low_ref.xlow_ref = bf16[5,32,1024]{2,1,0:T(8,128)(2,1)S(1)} collective-permute-done((bf16[5,32,1024]{2,1,0:T(8,128)(2,1)S(1)}, bf16[5,32,1024]{2,1,0:T(8,128)(2,1)S(1)}, u32[]{:S(2)}, u32[]{:S(2)}) %collective-permute-start) | collective-permute-done | bytes 327712 | tf_op jit(solution)/shard_map/ppermute | solution.py:639
  14.7 3.9 %collective-permute-done.1.high_ref.xhigh_ref = bf16[5,32,1024]{2,1,0:T(8,128)(2,1)S(1)} collective-permute-done((bf16[5,32,1024]{2,1,0:T(8,128)(2,1)S(1)}, bf16[5,32,1024]{2,1,0:T(8,128)(2,1)S(1)}, u32[]{:S(2)}, u32[]{:S(2)}) %collective-permute-start.1) | collective-permute-done | bytes 327712 | tf_op jit(solution)/shard_map/ppermute | solution.py:640
  18.5 1.1 shard_map.155
  19.6 3.9 %collective-permute-start.2 = (bf16[58,32,128]{2,1,0:T(8,128)(2,1)}, bf16[58,32,128]{2,1,0:T(8,128)(2,1)}, u32[]{:S(2)}, u32[]{:S(2)}) collective-permute-start(bf16[58,32,128]{2,1,0:T(8,128)(2,1)} %get-tuple-element.47), channel_id=1, source_target_pairs={{0,1},{1,2},{2,3},{4,5},{5,6},{6,7},{8,9},{9,10},{10,11},{12,13},{... | collective-permute-start | bytes 1425416 | tf_op jit(solution)/shard_map/ppermute | solution.py:644
  23.5 1.3 %collective-permute-start.3 = (bf16[58,32,128]{2,1,0:T(8,128)(2,1)}, bf16[58,32,128]{2,1,0:T(8,128)(2,1)}, u32[]{:S(2)}, u32[]{:S(2)}) collective-permute-start(bf16[58,32,128]{2,1,0:T(8,128)(2,1)} %get-tuple-element.48), channel_id=1, source_target_pairs={{1,0},{2,1},{3,2},{5,4},{6,5},{7,6},{9,8},{10,9},{11,10},{13,12},{... | collective-permute-start | bytes 1425416 | tf_op jit(solution)/shard_map/ppermute | solution.py:645
  24.8 16.8 %all-to-all-start = ((f32[256,1,128]{2,1,0:T(1,128)}), f32[256,1,128]{2,1,0:T(1,128)S(1)}, u32[]{:S(2)}, u32[]{:S(2)}) async-start(f32[256,1,128]{2,1,0:T(1,128)} %get-tuple-element.37), calls=%async_computation | async-start | bytes 262144 | tf_op jit(solution)/shard_map/all_to_all | solution.py:599
  41.6 0.1 pad_add_fusion.pos_ref.mask_ref
  41.7 0.1 pad_maximum_fusion
  41.8 12.8 %all-to-all-done.got_ref = f32[256,1,128]{2,1,0:T(1,128)S(1)} async-done(((f32[256,1,128]{2,1,0:T(1,128)}), f32[256,1,128]{2,1,0:T(1,128)S(1)}, u32[]{:S(2)}, u32[]{:S(2)}) %all-to-all-start) | async-done | bytes 131104 | tf_op jit(solution)/shard_map/all_to_all | solution.py:599
  54.6 0.1 broadcast_in_dim.4.par_ref
  54.7 1.8 %shard_map.154 = (f32[256,1,128]{2,1,0:T(1,128)}, f32[8,128]{1,0:T(8,128)S(1)}, f32[8,32,1024]{2,1,0:T(8,128)S(1)}) custom-call(f32[256,1,128]{2,1,0:T(1,128)S(1)} %all-to-all-done.got_ref, f32[128,128]{1,0:T(8,128)S(1)} %broadcast_in_dim.4.par_ref, bf16[8,32,1024]{2,1,0:T(8,128)(2,1)S(1)} %get-tuple-element.38.c2_ref, ...), custom_call_target="tpu_custom_call" | custom-call | bytes 1048576 | tf_op jit(solution)/shard_map/pallas_call | solution.py:75
  56.5 5.5 %all-to-all-start.1 = ((f32[256,1,128]{2,1,0:T(1,128)}), f32[256,1,128]{2,1,0:T(1,128)S(1)}, u32[]{:S(2)}, u32[]{:S(2)}) async-start(f32[256,1,128]{2,1,0:T(1,128)} %get-tuple-element.40), calls=%async_computation.1 | async-start | bytes 262144 | tf_op jit(solution)/shard_map/all_to_all | solution.py:599
  62.0 0.0 collective-permute-done.3.yhigh_in
  62.0 0.0 copy-start
  62.0 6.0 %shard_map.156 = (bf16[10,32,1280]{2,1,0:T(8,128)(2,1)}, bf16[12,32,1536]{2,1,0:T(8,128)(2,1)}, f32[12,32,1536]{2,1,0:T(8,128)}, f32[10,32,1280]{2,1,0:T(8,128)}...) custom-call(s32[2]{0:T(128)S(1)} %pad_add_fusion.pos_ref.mask_ref, f32[8,128]{1,0:T(8,128)S(1)} %get-tuple-element.41.stat_ref, ...), custom_call_target="tpu_custom_call" | custom-call | flops 5000000000 | bytes 1048576 | tf_op jit(solution)/shard_map/pallas_call | solution.py:75
  68.0 7.1 %all-to-all-done.1.got_ref = f32[256,1,128]{2,1,0:T(1,128)S(1)} async-done(((f32[256,1,128]{2,1,0:T(1,128)}), f32[256,1,128]{2,1,0:T(1,128)S(1)}, u32[]{:S(2)}, u32[]{:S(2)}) %all-to-all-start.1) | async-done | bytes 131104 | tf_op jit(solution)/shard_map/all_to_all | solution.py:599
  75.1 9.1 %shard_map.157 = (bf16[32,24,128]{2,1,0:T(8,128)(2,1)S(1)}, bf16[10,32,1280]{2,1,0:T(8,128)(2,1)S(1)}, f32[8,128]{1,0:T(8,128)S(1)}) custom-call(s32[2]{0:T(128)S(1)} %pad_add_fusion.pos_ref.mask_ref, f32[256,1,128]{2,1,0:T(1,128)S(1)} %all-to-all-done.1.got_ref, f32[8,128]{1,0:T(8,128)S(1)} %get-tuple-element.41.stat_ref, ...), custom_call_target="tpu_custom_call" | custom-call | flops 4000000000 | bytes 1048576 | tf_op jit(solution)/shard_map/pallas_call | solution.py:75
  84.3 11.5 %all_to_all.25.got_ref = bf16[32,24,128]{2,1,0:T(8,128)(2,1)S(1)} all-to-all(bf16[32,24,128]{2,1,0:T(8,128)(2,1)S(1)} %get-tuple-element.55), channel_id=1, replica_groups=mesh['dp_0'=8,'dp_1'=2,'sx'=4,'sy'=4] {'dp_1','sx','sy'}, dimensions={0} | all-to-all | bytes 393216 | tf_op jit(solution)/shard_map/all_to_all | solution.py:599
  95.8 0.2 shard_map.158
  96.0 11.2 %all_to_all.26.got_ref = bf16[8,24,128]{2,1,0:T(8,128)(2,1)S(1)} all-to-all(bf16[8,24,128]{2,1,0:T(8,128)(2,1)S(1)} %shard_map.158), channel_id=1, replica_groups=mesh['dp_0'=8,'dp_1'=2,'sx'=4,'sy'=4] {'dp_0'}, dimensions={0} | all-to-all | bytes 98304 | tf_op jit(solution)/shard_map/all_to_all | solution.py:599
  107.2 1.0 shard_map.159
  108.1 5.5 %all-to-all-start.4 = ((bf16[32,16,128]{2,1,0:T(8,128)(2,1)}), bf16[32,16,128]{2,1,0:T(8,128)(2,1)S(1)}, u32[]{:S(2)}, u32[]{:S(2)}) async-start(bf16[32,16,128]{2,1,0:T(8,128)(2,1)} %get-tuple-element.60), calls=%async_computation.4 | async-start | bytes 262144 | tf_op jit(solution)/shard_map/all_to_all | solution.py:599
  113.7 4.8 %shard_map.160 = (bf16[1,32,8,8,128]{4,3,2,1,0:T(8,128)(2,1)}, f32[1,32]{1,0:T(1,128)}, f32[1,32]{1,0:T(1,128)}, f32[1,32]{1,0:T(1,128)}, f32[1,32]{1,0:T(1,128)}) custom-call(s32[2]{0:T(128)S(1)} %pad_add_fusion.pos_ref.mask_ref, f32[8,128]{1,0:T(8,128)S(1)} %get-tuple-element.56.sum_ref, f32[8,128]{1,0:T(8,128)S(1)} %get-tuple-element.57.two_ref, ...), custom_call_target="tpu_custom_call" | custom-call | flops 4000000000 | bytes 1048576 | tf_op jit(solution)/shard_map/pallas_call | solution.py:75
  118.5 2.7 %all-to-all-done.4.got_ref = bf16[32,16,128]{2,1,0:T(8,128)(2,1)S(1)} async-done(((bf16[32,16,128]{2,1,0:T(8,128)(2,1)}), bf16[32,16,128]{2,1,0:T(8,128)(2,1)S(1)}, u32[]{:S(2)}, u32[]{:S(2)}) %all-to-all-start.4) | async-done | bytes 131104 | tf_op jit(solution)/shard_map/all_to_all | solution.py:599
  121.2 1.1 shard_map.161
  (9 shorter events, 0.0 us)
Async XLA Ops:
  4.1 37.6 %copy-start.2 = (f32[32]{0:T(128)S(1)}, f32[32]{0:T(128)}, u32[]{:S(2)}) copy-start(f32[32]{0:T(128)} %param.19) | copy-start | bytes 388
  4.1 37.6 %copy-start.3 = (f32[32]{0:T(128)S(1)}, f32[32]{0:T(128)}, u32[]{:S(2)}) copy-start(f32[32]{0:T(128)} %param.18) | copy-start | bytes 388
  4.1 37.6 %copy-start.4 = (f32[32]{0:T(128)S(1)}, f32[32]{0:T(128)}, u32[]{:S(2)}) copy-start(f32[32]{0:T(128)} %param.17) | copy-start | bytes 388
  4.1 37.6 %copy-start.5 = (f32[32]{0:T(128)S(1)}, f32[32]{0:T(128)}, u32[]{:S(2)}) copy-start(f32[32]{0:T(128)} %param.16) | copy-start | bytes 388
  4.1 10.5 %collective-permute-start = (bf16[5,32,1024]{2,1,0:T(8,128)(2,1)S(1)}, bf16[5,32,1024]{2,1,0:T(8,128)(2,1)S(1)}, u32[]{:S(2)}, u32[]{:S(2)}) collective-permute-start(bf16[5,32,1024]{2,1,0:T(8,128)(2,1)S(1)} %get-tuple-element.44), channel_id=1, source_target_pairs={{0,4},{4,8},{8,12},{1,5},{5,9},{9,13},{2,6},{6,10},{10,14},{3,7},{... | collective-permute-start | bytes 983048 | tf_op jit(solution)/shard_map/ppermute | solution.py:639
  8.3 10.2 %collective-permute-start.1 = (bf16[5,32,1024]{2,1,0:T(8,128)(2,1)S(1)}, bf16[5,32,1024]{2,1,0:T(8,128)(2,1)S(1)}, u32[]{:S(2)}, u32[]{:S(2)}) collective-permute-start(bf16[5,32,1024]{2,1,0:T(8,128)(2,1)S(1)} %get-tuple-element.45), channel_id=1, source_target_pairs={{4,0},{8,4},{12,8},{5,1},{9,5},{13,9},{6,2},{10,6},{14,10},{7,3},{... | collective-permute-start | bytes 983048 | tf_op jit(solution)/shard_map/ppermute | solution.py:640
  19.6 42.4 %collective-permute-start.2 = (bf16[58,32,128]{2,1,0:T(8,128)(2,1)}, bf16[58,32,128]{2,1,0:T(8,128)(2,1)}, u32[]{:S(2)}, u32[]{:S(2)}) collective-permute-start(bf16[58,32,128]{2,1,0:T(8,128)(2,1)} %get-tuple-element.47), channel_id=1, source_target_pairs={{0,1},{1,2},{2,3},{4,5},{5,6},{6,7},{8,9},{9,10},{10,11},{12,13},{... | collective-permute-start | bytes 1425416 | tf_op jit(solution)/shard_map/ppermute | solution.py:644
  23.5 38.5 %collective-permute-start.3 = (bf16[58,32,128]{2,1,0:T(8,128)(2,1)}, bf16[58,32,128]{2,1,0:T(8,128)(2,1)}, u32[]{:S(2)}, u32[]{:S(2)}) collective-permute-start(bf16[58,32,128]{2,1,0:T(8,128)(2,1)} %get-tuple-element.48), channel_id=1, source_target_pairs={{1,0},{2,1},{3,2},{5,4},{6,5},{7,6},{9,8},{10,9},{11,10},{13,12},{... | collective-permute-start | bytes 1425416 | tf_op jit(solution)/shard_map/ppermute | solution.py:645
  24.8 29.8 %all-to-all-start = ((f32[256,1,128]{2,1,0:T(1,128)}), f32[256,1,128]{2,1,0:T(1,128)S(1)}, u32[]{:S(2)}, u32[]{:S(2)}) async-start(f32[256,1,128]{2,1,0:T(1,128)} %get-tuple-element.37), calls=%async_computation | async-start | bytes 262144 | tf_op jit(solution)/shard_map/all_to_all | solution.py:599
  56.5 18.7 %all-to-all-start.1 = ((f32[256,1,128]{2,1,0:T(1,128)}), f32[256,1,128]{2,1,0:T(1,128)S(1)}, u32[]{:S(2)}, u32[]{:S(2)}) async-start(f32[256,1,128]{2,1,0:T(1,128)} %get-tuple-element.40), calls=%async_computation.1 | async-start | bytes 262144 | tf_op jit(solution)/shard_map/all_to_all | solution.py:599
  62.0 13.1 %copy-start = (bf16[3,3,3,32,32]{4,3,2,1,0:T(8,128)(2,1)S(1)}, bf16[3,3,3,32,32]{4,3,2,1,0:T(8,128)(2,1)}, u32[]{:S(2)}) copy-start(bf16[3,3,3,32,32]{4,3,2,1,0:T(8,128)(2,1)} %raw.2) | copy-start | bytes 165892
  75.1 38.6 %copy-start.1 = (bf16[3,3,3,32,32]{4,3,2,1,0:T(8,128)(2,1)S(1)}, bf16[3,3,3,32,32]{4,3,2,1,0:T(8,128)(2,1)}, u32[]{:S(2)}) copy-start(bf16[3,3,3,32,32]{4,3,2,1,0:T(8,128)(2,1)} %raw.3) | copy-start | bytes 165892
  108.1 13.1 %all-to-all-start.4 = ((bf16[32,16,128]{2,1,0:T(8,128)(2,1)}), bf16[32,16,128]{2,1,0:T(8,128)(2,1)S(1)}, u32[]{:S(2)}, u32[]{:S(2)}) async-start(bf16[32,16,128]{2,1,0:T(8,128)(2,1)} %get-tuple-element.60), calls=%async_computation.4 | async-start | bytes 262144 | tf_op jit(solution)/shard_map/all_to_all | solution.py:599

commit v4 on v3

--- a/solution.py
+++ b/solution.py
@@ -123,13 +123,18 @@
     held, vol3, sems, out_sem,
 ):
     sources = (("vol", vol_ref, None), ("c1", one_ref, c1_ref), ("c2", two_ref, c2_ref), ("ug", up_ref, ug_ref))
-    copies = started([(src.at[0], held.at[n]) for n, (_, src, _) in enumerate(sources)], sems)
+    half = [pl.ds(n * (B // 2), B // 2) for n in range(2)]
+    halves = started([(vol_ref.at[0, :, cut], held.at[0, :, cut]) for cut in half], sems.at[pl.ds(3, 2)])
+    copies = started([(src.at[0], held.at[n + 1]) for n, (_, src, _) in enumerate(sources[1:])], sems)
     lane = lanes()
     parts = []
     for n, (name, _, dst) in enumerate(sources):
-        copies[n].wait()
+        if n > 0:
+            copies[n - 1].wait()
         total, squares = jnp.zeros((C, Z), F32), jnp.zeros((C, Z), F32)
         for x in range(B):
+            if n == 0 and x % (B // 2) == 0:
+                halves[x // (B // 2)].wait()
             turned_x = jnp.swapaxes(held[n, :, x].astype(F32), 0, 1)
             for y in range(B):
                 slab = turned_x[y]
@@ -317,7 +322,7 @@
         return b, g
 
     zero = jnp.zeros((C, Z), F32)
-    b, g = lax.fori_loop(0, B, body, (zero, zero))
+    b, g = lax.fori_loop(0, B, body, (zero, zero), unroll=4)
     out = across(jnp.concatenate([b, g, zero, zero], 0))
     out_ref[...] = jnp.broadcast_to(out[None], out_ref.shape)
 
@@ -627,7 +632,7 @@
         scratch=[
             pltpu.VMEM((4, C, B, B, Z), BF16),
             room(three_fold),
-            sems(4),
+            sems(5),
             sems(1),
         ],
         spaces=[HBM] * 4,

time: 123 us -> 123 us (level)
  no operation moved by 1% of the time
where the time goes in v4:
time: 123 us; the launch traced here: 122 us
  starting transfers between devices  38.5 us (31%)
  waiting for transfers between devices  31.6 us (26%)
  Pallas kernels  28.3 us (23%)
  blocking collectives  22.7 us (18%)
    pallas_call x9, Pallas kernels, placed(): f(*[pltpu.with_memory_space_constraint(x, HBM) if space == HBM else x for...  28.3 us
    all_to_all x3, starting transfers between devices, exchanged(): return lax.all_to_all(array, axes, 0, 0, tiled=True)  27.9 us
    all_to_all x2, blocking collectives, exchanged(): return lax.all_to_all(array, axes, 0, 0, tiled=True)  22.7 us
    all_to_all x3, waiting for transfers between devices, exchanged(): return lax.all_to_all(array, axes, 0, 0, tiled=True)  22.7 us
    ppermute x1, waiting for transfers between devices, per_device(): x_low = lax.ppermute(send_up, 'sx', up)  5.06 us
    ppermute x1, starting transfers between devices, per_device(): x_low = lax.ppermute(send_up, 'sx', up)  4.17 us
    ppermute x1, starting transfers between devices, per_device(): y_low = lax.ppermute(send_up, 'sy', up)  3.88 us
    ppermute x1, waiting for transfers between devices, per_device(): x_high = lax.ppermute(send_down, 'sx', down_)  3.85 us
  transfers between devices with their start and end apart: 7, of which 5 were waited for; matrix products, arithmetic and copies ran while one was open for 0% of the time, Pallas kernels for 10%

profile of v4, /device:TPU:1, one launch (start us, length us, event | category | flops | bytes accessed | tf_op | source)
XLA Modules:
  0.0 122.2 jit_solution(8982342786891950296)
XLA Ops:
  0.6 3.4 %shard_map.153 = (bf16[8,32,1024]{2,1,0:T(8,128)(2,1)S(1)}, bf16[8,32,1024]{2,1,0:T(8,128)(2,1)S(1)}, bf16[8,32,1024]{2,1,0:T(8,128)(2,1)S(1)}, bf16[8,96,1024]{...) custom-call(bf16[1,32,8,8,128]{4,3,2,1,0:T(8,128)(2,1)} %one_ref.1, ...), custom_call_target="tpu_custom_call" | custom-call | bytes 1048576 | tf_op jit(solution)/shard_map/pallas_call | solution.py:75
  4.0 0.0 copy-start.2
  4.0 0.0 copy-start.3
  4.0 0.0 copy-start.4
  4.1 0.0 copy-start.5
  4.1 4.2 %collective-permute-start = (bf16[5,32,1024]{2,1,0:T(8,128)(2,1)S(1)}, bf16[5,32,1024]{2,1,0:T(8,128)(2,1)S(1)}, u32[]{:S(2)}, u32[]{:S(2)}) collective-permute-start(bf16[5,32,1024]{2,1,0:T(8,128)(2,1)S(1)} %get-tuple-element.44), channel_id=1, source_target_pairs={{0,4},{4,8},{8,12},{1,5},{5,9},{9,13},{2,6},{6,10},{10,14},{3,7},{... | collective-permute-start | bytes 983048 | tf_op jit(solution)/shard_map/ppermute | solution.py:644
  8.2 1.3 %collective-permute-start.1 = (bf16[5,32,1024]{2,1,0:T(8,128)(2,1)S(1)}, bf16[5,32,1024]{2,1,0:T(8,128)(2,1)S(1)}, u32[]{:S(2)}, u32[]{:S(2)}) collective-permute-start(bf16[5,32,1024]{2,1,0:T(8,128)(2,1)S(1)} %get-tuple-element.45), channel_id=1, source_target_pairs={{4,0},{8,4},{12,8},{5,1},{9,5},{13,9},{6,2},{10,6},{14,10},{7,3},{... | collective-permute-start | bytes 983048 | tf_op jit(solution)/shard_map/ppermute | solution.py:645
  9.5 5.1 %collective-permute-done.low_ref.xlow_ref = bf16[5,32,1024]{2,1,0:T(8,128)(2,1)S(1)} collective-permute-done((bf16[5,32,1024]{2,1,0:T(8,128)(2,1)S(1)}, bf16[5,32,1024]{2,1,0:T(8,128)(2,1)S(1)}, u32[]{:S(2)}, u32[]{:S(2)}) %collective-permute-start) | collective-permute-done | bytes 327712 | tf_op jit(solution)/shard_map/ppermute | solution.py:644
  14.6 3.9 %collective-permute-done.1.high_ref.xhigh_ref = bf16[5,32,1024]{2,1,0:T(8,128)(2,1)S(1)} collective-permute-done((bf16[5,32,1024]{2,1,0:T(8,128)(2,1)S(1)}, bf16[5,32,1024]{2,1,0:T(8,128)(2,1)S(1)}, u32[]{:S(2)}, u32[]{:S(2)}) %collective-permute-start.1) | collective-permute-done | bytes 327712 | tf_op jit(solution)/shard_map/ppermute | solution.py:645
  18.5 1.1 shard_map.155
  19.6 3.9 %collective-permute-start.2 = (bf16[58,32,128]{2,1,0:T(8,128)(2,1)}, bf16[58,32,128]{2,1,0:T(8,128)(2,1)}, u32[]{:S(2)}, u32[]{:S(2)}) collective-permute-start(bf16[58,32,128]{2,1,0:T(8,128)(2,1)} %get-tuple-element.47), channel_id=1, source_target_pairs={{0,1},{1,2},{2,3},{4,5},{5,6},{6,7},{8,9},{9,10},{10,11},{12,13},{... | collective-permute-start | bytes 1425416 | tf_op jit(solution)/shard_map/ppermute | solution.py:649
  23.4 1.3 %collective-permute-start.3 = (bf16[58,32,128]{2,1,0:T(8,128)(2,1)}, bf16[58,32,128]{2,1,0:T(8,128)(2,1)}, u32[]{:S(2)}, u32[]{:S(2)}) collective-permute-start(bf16[58,32,128]{2,1,0:T(8,128)(2,1)} %get-tuple-element.48), channel_id=1, source_target_pairs={{1,0},{2,1},{3,2},{5,4},{6,5},{7,6},{9,8},{10,9},{11,10},{13,12},{... | collective-permute-start | bytes 1425416 | tf_op jit(solution)/shard_map/ppermute | solution.py:650
  24.7 16.8 %all-to-all-start = ((f32[256,1,128]{2,1,0:T(1,128)}), f32[256,1,128]{2,1,0:T(1,128)S(1)}, u32[]{:S(2)}, u32[]{:S(2)}) async-start(f32[256,1,128]{2,1,0:T(1,128)} %get-tuple-element.37), calls=%async_computation | async-start | bytes 262144 | tf_op jit(solution)/shard_map/all_to_all | solution.py:604
  41.6 0.1 pad_add_fusion.pos_ref.mask_ref
  41.7 0.1 pad_maximum_fusion
  41.7 12.8 %all-to-all-done.got_ref = f32[256,1,128]{2,1,0:T(1,128)S(1)} async-done(((f32[256,1,128]{2,1,0:T(1,128)}), f32[256,1,128]{2,1,0:T(1,128)S(1)}, u32[]{:S(2)}, u32[]{:S(2)}) %all-to-all-start) | async-done | bytes 131104 | tf_op jit(solution)/shard_map/all_to_all | solution.py:604
  54.6 0.1 broadcast_in_dim.4.par_ref
  54.6 1.7 %shard_map.154 = (f32[256,1,128]{2,1,0:T(1,128)}, f32[8,128]{1,0:T(8,128)S(1)}, f32[8,32,1024]{2,1,0:T(8,128)S(1)}) custom-call(f32[256,1,128]{2,1,0:T(1,128)S(1)} %all-to-all-done.got_ref, f32[128,128]{1,0:T(8,128)S(1)} %broadcast_in_dim.4.par_ref, bf16[8,32,1024]{2,1,0:T(8,128)(2,1)S(1)} %get-tuple-element.38.c2_ref, ...), custom_call_target="tpu_custom_call" | custom-call | bytes 1048576 | tf_op jit(solution)/shard_map/pallas_call | solution.py:75
  56.3 5.5 %all-to-all-start.1 = ((f32[256,1,128]{2,1,0:T(1,128)}), f32[256,1,128]{2,1,0:T(1,128)S(1)}, u32[]{:S(2)}, u32[]{:S(2)}) async-start(f32[256,1,128]{2,1,0:T(1,128)} %get-tuple-element.40), calls=%async_computation.1 | async-start | bytes 262144 | tf_op jit(solution)/shard_map/all_to_all | solution.py:604
  61.9 0.0 collective-permute-done.3.yhigh_in
  61.9 0.0 copy-start
  61.9 6.0 %shard_map.156 = (bf16[10,32,1280]{2,1,0:T(8,128)(2,1)}, bf16[12,32,1536]{2,1,0:T(8,128)(2,1)}, f32[12,32,1536]{2,1,0:T(8,128)}, f32[10,32,1280]{2,1,0:T(8,128)}...) custom-call(s32[2]{0:T(128)S(1)} %pad_add_fusion.pos_ref.mask_ref, f32[8,128]{1,0:T(8,128)S(1)} %get-tuple-element.41.stat_ref, ...), custom_call_target="tpu_custom_call" | custom-call | flops 5000000000 | bytes 1048576 | tf_op jit(solution)/shard_map/pallas_call | solution.py:75
  67.9 7.1 %all-to-all-done.1.got_ref = f32[256,1,128]{2,1,0:T(1,128)S(1)} async-done(((f32[256,1,128]{2,1,0:T(1,128)}), f32[256,1,128]{2,1,0:T(1,128)S(1)}, u32[]{:S(2)}, u32[]{:S(2)}) %all-to-all-start.1) | async-done | bytes 131104 | tf_op jit(solution)/shard_map/all_to_all | solution.py:604
  75.0 9.1 %shard_map.157 = (bf16[32,24,128]{2,1,0:T(8,128)(2,1)S(1)}, bf16[10,32,1280]{2,1,0:T(8,128)(2,1)S(1)}, f32[8,128]{1,0:T(8,128)S(1)}) custom-call(s32[2]{0:T(128)S(1)} %pad_add_fusion.pos_ref.mask_ref, f32[256,1,128]{2,1,0:T(1,128)S(1)} %all-to-all-done.1.got_ref, f32[8,128]{1,0:T(8,128)S(1)} %get-tuple-element.41.stat_ref, ...), custom_call_target="tpu_custom_call" | custom-call | flops 4000000000 | bytes 1048576 | tf_op jit(solution)/shard_map/pallas_call | solution.py:75
  84.1 11.5 %all_to_all.25.got_ref = bf16[32,24,128]{2,1,0:T(8,128)(2,1)S(1)} all-to-all(bf16[32,24,128]{2,1,0:T(8,128)(2,1)S(1)} %get-tuple-element.55), channel_id=1, replica_groups=mesh['dp_0'=8,'dp_1'=2,'sx'=4,'sy'=4] {'dp_1','sx','sy'}, dimensions={0} | all-to-all | bytes 393216 | tf_op jit(solution)/shard_map/all_to_all | solution.py:604
  95.7 0.2 shard_map.158
  95.9 11.2 %all_to_all.26.got_ref = bf16[8,24,128]{2,1,0:T(8,128)(2,1)S(1)} all-to-all(bf16[8,24,128]{2,1,0:T(8,128)(2,1)S(1)} %shard_map.158), channel_id=1, replica_groups=mesh['dp_0'=8,'dp_1'=2,'sx'=4,'sy'=4] {'dp_0'}, dimensions={0} | all-to-all | bytes 98304 | tf_op jit(solution)/shard_map/all_to_all | solution.py:604
  107.0 1.0 shard_map.159
  108.0 5.5 %all-to-all-start.4 = ((bf16[32,16,128]{2,1,0:T(8,128)(2,1)}), bf16[32,16,128]{2,1,0:T(8,128)(2,1)S(1)}, u32[]{:S(2)}, u32[]{:S(2)}) async-start(bf16[32,16,128]{2,1,0:T(8,128)(2,1)} %get-tuple-element.60), calls=%async_computation.4 | async-start | bytes 262144 | tf_op jit(solution)/shard_map/all_to_all | solution.py:604
  113.6 4.8 %shard_map.160 = (bf16[1,32,8,8,128]{4,3,2,1,0:T(8,128)(2,1)}, f32[1,32]{1,0:T(1,128)}, f32[1,32]{1,0:T(1,128)}, f32[1,32]{1,0:T(1,128)}, f32[1,32]{1,0:T(1,128)}) custom-call(s32[2]{0:T(128)S(1)} %pad_add_fusion.pos_ref.mask_ref, f32[8,128]{1,0:T(8,128)S(1)} %get-tuple-element.56.sum_ref, f32[8,128]{1,0:T(8,128)S(1)} %get-tuple-element.57.two_ref, ...), custom_call_target="tpu_custom_call" | custom-call | flops 4000000000 | bytes 1048576 | tf_op jit(solution)/shard_map/pallas_call | solution.py:75
  118.4 2.7 %all-to-all-done.4.got_ref = bf16[32,16,128]{2,1,0:T(8,128)(2,1)S(1)} async-done(((bf16[32,16,128]{2,1,0:T(8,128)(2,1)}), bf16[32,16,128]{2,1,0:T(8,128)(2,1)S(1)}, u32[]{:S(2)}, u32[]{:S(2)}) %all-to-all-start.4) | async-done | bytes 131104 | tf_op jit(solution)/shard_map/all_to_all | solution.py:604
  121.1 1.1 shard_map.161
  (9 shorter events, 0.0 us)
Async XLA Ops:
  4.0 37.6 %copy-start.2 = (f32[32]{0:T(128)S(1)}, f32[32]{0:T(128)}, u32[]{:S(2)}) copy-start(f32[32]{0:T(128)} %param.19) | copy-start | bytes 388
  4.0 37.6 %copy-start.3 = (f32[32]{0:T(128)S(1)}, f32[32]{0:T(128)}, u32[]{:S(2)}) copy-start(f32[32]{0:T(128)} %param.18) | copy-start | bytes 388
  4.0 37.6 %copy-start.4 = (f32[32]{0:T(128)S(1)}, f32[32]{0:T(128)}, u32[]{:S(2)}) copy-start(f32[32]{0:T(128)} %param.17) | copy-start | bytes 388
  4.1 37.6 %copy-start.5 = (f32[32]{0:T(128)S(1)}, f32[32]{0:T(128)}, u32[]{:S(2)}) copy-start(f32[32]{0:T(128)} %param.16) | copy-start | bytes 388
  4.1 10.5 %collective-permute-start = (bf16[5,32,1024]{2,1,0:T(8,128)(2,1)S(1)}, bf16[5,32,1024]{2,1,0:T(8,128)(2,1)S(1)}, u32[]{:S(2)}, u32[]{:S(2)}) collective-permute-start(bf16[5,32,1024]{2,1,0:T(8,128)(2,1)S(1)} %get-tuple-element.44), channel_id=1, source_target_pairs={{0,4},{4,8},{8,12},{1,5},{5,9},{9,13},{2,6},{6,10},{10,14},{3,7},{... | collective-permute-start | bytes 983048 | tf_op jit(solution)/shard_map/ppermute | solution.py:644
  8.2 10.2 %collective-permute-start.1 = (bf16[5,32,1024]{2,1,0:T(8,128)(2,1)S(1)}, bf16[5,32,1024]{2,1,0:T(8,128)(2,1)S(1)}, u32[]{:S(2)}, u32[]{:S(2)}) collective-permute-start(bf16[5,32,1024]{2,1,0:T(8,128)(2,1)S(1)} %get-tuple-element.45), channel_id=1, source_target_pairs={{4,0},{8,4},{12,8},{5,1},{9,5},{13,9},{6,2},{10,6},{14,10},{7,3},{... | collective-permute-start | bytes 983048 | tf_op jit(solution)/shard_map/ppermute | solution.py:645
  19.6 42.3 %collective-permute-start.2 = (bf16[58,32,128]{2,1,0:T(8,128)(2,1)}, bf16[58,32,128]{2,1,0:T(8,128)(2,1)}, u32[]{:S(2)}, u32[]{:S(2)}) collective-permute-start(bf16[58,32,128]{2,1,0:T(8,128)(2,1)} %get-tuple-element.47), channel_id=1, source_target_pairs={{0,1},{1,2},{2,3},{4,5},{5,6},{6,7},{8,9},{9,10},{10,11},{12,13},{... | collective-permute-start | bytes 1425416 | tf_op jit(solution)/shard_map/ppermute | solution.py:649
  23.4 38.5 %collective-permute-start.3 = (bf16[58,32,128]{2,1,0:T(8,128)(2,1)}, bf16[58,32,128]{2,1,0:T(8,128)(2,1)}, u32[]{:S(2)}, u32[]{:S(2)}) collective-permute-start(bf16[58,32,128]{2,1,0:T(8,128)(2,1)} %get-tuple-element.48), channel_id=1, source_target_pairs={{1,0},{2,1},{3,2},{5,4},{6,5},{7,6},{9,8},{10,9},{11,10},{13,12},{... | collective-permute-start | bytes 1425416 | tf_op jit(solution)/shard_map/ppermute | solution.py:650
  24.7 29.8 %all-to-all-start = ((f32[256,1,128]{2,1,0:T(1,128)}), f32[256,1,128]{2,1,0:T(1,128)S(1)}, u32[]{:S(2)}, u32[]{:S(2)}) async-start(f32[256,1,128]{2,1,0:T(1,128)} %get-tuple-element.37), calls=%async_computation | async-start | bytes 262144 | tf_op jit(solution)/shard_map/all_to_all | solution.py:604
  56.3 18.7 %all-to-all-start.1 = ((f32[256,1,128]{2,1,0:T(1,128)}), f32[256,1,128]{2,1,0:T(1,128)S(1)}, u32[]{:S(2)}, u32[]{:S(2)}) async-start(f32[256,1,128]{2,1,0:T(1,128)} %get-tuple-element.40), calls=%async_computation.1 | async-start | bytes 262144 | tf_op jit(solution)/shard_map/all_to_all | solution.py:604
  61.9 13.1 %copy-start = (bf16[3,3,3,32,32]{4,3,2,1,0:T(8,128)(2,1)S(1)}, bf16[3,3,3,32,32]{4,3,2,1,0:T(8,128)(2,1)}, u32[]{:S(2)}) copy-start(bf16[3,3,3,32,32]{4,3,2,1,0:T(8,128)(2,1)} %raw.2) | copy-start | bytes 165892
  75.0 38.6 %copy-start.1 = (bf16[3,3,3,32,32]{4,3,2,1,0:T(8,128)(2,1)S(1)}, bf16[3,3,3,32,32]{4,3,2,1,0:T(8,128)(2,1)}, u32[]{:S(2)}) copy-start(bf16[3,3,3,32,32]{4,3,2,1,0:T(8,128)(2,1)} %raw.3) | copy-start | bytes 165892
  108.0 13.1 %all-to-all-start.4 = ((bf16[32,16,128]{2,1,0:T(8,128)(2,1)}), bf16[32,16,128]{2,1,0:T(8,128)(2,1)S(1)}, u32[]{:S(2)}, u32[]{:S(2)}) async-start(bf16[32,16,128]{2,1,0:T(8,128)(2,1)} %get-tuple-element.60), calls=%async_computation.4 | async-start | bytes 262144 | tf_op jit(solution)/shard_map/all_to_all | solution.py:604
